TPU v7x, 128 devices: a whole 4x4x4 slice. The times are simulated.
128 devices in a mesh: lat: 32 (over z, x, core), fld: 4 (over y).
Axes of the slice: x: 4, y: 4, z: 4, core: 2. Of those that a mesh axis runs over, the one named last changes fastest.
Arguments:
- grid_in: bfloat16 [32, 2560, 2688], P('fld', 'lat'), may hold values from -6 to 6
- legendre: bfloat16 [768, 1280, 768], P(('lat', 'fld')), may hold values from -0.15625 to 0.15625
- wave_slot: int32 [768], replicated, may hold values from 512 to 1279, as said below
- lat_modes: int32 [2560], P('lat'), may hold values from 10 to 1280
- gauss_weight: float32 [1280], replicated, may hold values from 0.5 to 2
- diffusion: float32 [32], replicated, may hold values from 0.5 to 8
Outputs:
- grid_out: float32 [32, 2560, 2688], P('fld', 'lat')
- spectra: float32 [2, 768, 32, 768], P(None, 'lat', 'fld')
Inputs may be any that keep to these rules, and one draw needn't show every extreme that they name: `wave_slot`: every wavenumber from 512 to 1279 stands in exactly one slot; slots 2 t and 2 t + 1 hold two wavenumbers that sum to 1791, the smaller one in the even slot.
All inputs are finite; a program needn't handle non-finite values.
Results may differ from a plain program's by a relative error of at most 0.0071.
Values may be sent and summed in bfloat16 or wider, within the bound.
A program may use at most 192 MiB of HBM per device.

v0:
```python
import math

import jax
import jax.numpy as jnp
from jax import lax
from jax.sharding import PartitionSpec as P

LMAX = 1279


def split_up(value, dim, length):
    shape = value.shape
    parts = value.reshape(*shape[:dim], length, shape[dim] // length, *shape[dim + 1 :])
    return jnp.moveaxis(parts, dim, 0)


def laid_out(parts, dim):
    parts = jnp.moveaxis(parts, 0, dim)
    shape = parts.shape
    return parts.reshape(*shape[:dim], shape[dim] * shape[dim + 1], *shape[dim + 2 :])


def exchange_both(value, axis, axes, splits, concats):
    sizes = [lax.axis_size(a) for a in axes]
    parts = split_up(value, splits[0], sizes[0])
    parts = jnp.moveaxis(split_up(parts, splits[1] + 1, sizes[1]), 0, 1)
    inside = parts.shape[2:]
    parts = parts.reshape(-1, *inside)
    parts = lax.all_to_all(parts, axis, split_axis=0, concat_axis=0, tiled=True)
    parts = laid_out(parts.reshape(*sizes, *inside), concats[0] + 1)
    return laid_out(parts, concats[1])


def angle_table(waves, lon_count):
    points = jnp.arange(lon_count, dtype=jnp.int32)
    phase_index = points[:, None] * waves[None, :] % lon_count
    radians = phase_index.astype(jnp.float32) * (2.0 * math.pi / lon_count)
    norm_scale = 1.0 / math.sqrt(lon_count)
    return jnp.stack([jnp.cos(radians) * norm_scale, -jnp.sin(radians) * norm_scale], 1).astype(
        jnp.bfloat16
    )


def damping(waves, damp_rates, columns):
    half_cols = columns // 2
    col_index = jnp.arange(columns, dtype=jnp.int32)
    offset = jnp.where(col_index < half_cols, 2 * col_index, 2 * col_index - columns + 1)
    degree = waves[:, None] + offset[None, :]
    degree_ratio = (degree * (degree + 1)).astype(jnp.float32) / float(LMAX * (LMAX + 1))
    factor = 1.0 / (1.0 + damp_rates[None, :, None] * (degree_ratio**4)[:, None, :])
    return jnp.where((degree <= LMAX)[:, None, :], factor, 0.0)


def project(even_part, odd_part, tables, used_cols):
    half_cols = tables.shape[2] // 2
    even_cols = jnp.einsum(
        "rsfj,sjq->rsfq", even_part, tables[:, :, :used_cols], preferred_element_type=jnp.float32
    )
    odd_cols = jnp.einsum(
        "rsfj,sjq->rsfq",
        odd_part,
        tables[:, :, half_cols : half_cols + used_cols],
        preferred_element_type=jnp.float32,
    )
    return jnp.concatenate([even_cols, odd_cols], -1)


def expand(rounded, tables, used_cols):
    half_cols = tables.shape[2] // 2
    sym_part = jnp.einsum(
        "rsfq,sjq->rsfj",
        rounded[..., :used_cols],
        tables[:, :, :used_cols],
        preferred_element_type=jnp.float32,
    )
    anti_part = jnp.einsum(
        "rsfq,sjq->rsfj",
        rounded[..., half_cols : half_cols + used_cols],
        tables[:, :, half_cols : half_cols + used_cols],
        preferred_element_type=jnp.float32,
    )
    return (sym_part, anti_part)


def transform_block(block_data, tables, block_waves, damp_rates, weights):
    half_lats = weights.shape[0]
    columns = tables.shape[2]
    half_cols = columns // 2
    north_half = block_data[..., :half_lats].astype(jnp.float32)
    south_half = jnp.flip(block_data[..., half_lats:], -1).astype(jnp.float32)
    even_part = ((north_half + south_half) * weights).astype(jnp.bfloat16)
    odd_part = ((north_half - south_half) * weights).astype(jnp.bfloat16)
    raw_coeff = project(even_part, odd_part, tables, half_cols)
    spectra = raw_coeff * damping(block_waves, damp_rates, columns)[None]
    rounded = spectra.astype(jnp.bfloat16)
    sym_part, anti_part = expand(rounded, tables, half_cols)
    synthesized = jnp.concatenate(
        [
            (sym_part + anti_part).astype(jnp.bfloat16),
            jnp.flip((sym_part - anti_part).astype(jnp.bfloat16), -1),
        ],
        -1,
    )
    return (spectra, synthesized)


def body(grid_in, legendre, wave_slot, lat_modes, gauss_weight, diffusion):
    fld_dev, lat_dev, lon_count = grid_in.shape
    slots_all = wave_slot.shape[0]
    lat_count = lax.axis_size("lat")
    fld_count = lax.axis_size("fld")
    lat_index = lax.axis_index("lat")
    fld_index = lax.axis_index("fld")
    owned_slots = slots_all // (lat_count * fld_count)
    angles = angle_table(wave_slot, lon_count)
    keep_mask = (wave_slot[:, None] < lat_modes[None, :]).astype(jnp.float32)
    fourier = jnp.einsum("fjx,xrs->rsfj", grid_in, angles, preferred_element_type=jnp.float32)
    fourier = (fourier * keep_mask[None, :, None, :]).astype(jnp.bfloat16)
    own_waves = lax.dynamic_slice_in_dim(
        wave_slot, (lat_index * fld_count + fld_index) * owned_slots, owned_slots
    )
    arrived = exchange_both(fourier, ("lat", "fld"), ("lat", "fld"), (1, 1), (3, 2))
    owned_spectra, synthesized = transform_block(
        arrived, legendre, own_waves, diffusion, gauss_weight
    )
    spectra = lax.all_to_all(owned_spectra, "fld", split_axis=2, concat_axis=1, tiled=True)
    reordered = exchange_both(synthesized, ("lat", "fld"), ("lat", "fld"), (3, 2), (1, 1))
    returned = reordered.reshape(2, fld_count, lat_count, owned_slots, fld_dev, lat_dev)
    returned = returned.transpose(0, 2, 1, 3, 4, 5).reshape(2, slots_all, fld_dev, lat_dev)
    keep_narrow = keep_mask.astype(jnp.bfloat16)
    masked = returned * keep_narrow[None, :, None, :]
    grid_out = 2.0 * jnp.einsum("rsfj,xrs->fjx", masked, angles, preferred_element_type=jnp.float32)
    return (grid_out, spectra)


def solution(mesh):
    return jax.shard_map(
        body,
        mesh=mesh,
        in_specs=(P("fld", "lat", None), P(("lat", "fld"), None, None), P(), P("lat"), P(), P()),
        out_specs=(P("fld", "lat", None), P(None, "lat", "fld", None)),
        check_vma=False,
    )
```

profile of v0, /device:TPU:1, one launch (start us, length us, event | category | flops | bytes accessed | tf_op | source)
XLA Modules:
  0.0 228.5 jit_solution(8839677291289214991)
XLA Ops:
  0.6 0.0 copy-start
  0.7 36.8 %multiply_convert_fusion.1 = (bf16[2688,1,768]{2,0,1:T(8,128)(2,1)S(1)}, bf16[2688,1,768]{2,0,1:T(8,128)(2,1)S(1)}) fusion(s32[768]{0:T(1024)} %param.8), kind=kLoop, calls=%fused_computation.9 | loop fusion | flops 28901376 | bytes 8260608 | tf_op jit(solution)/shard_map/convert
  37.5 0.0 copy-start.5
  37.5 0.9 fusion.45
  38.4 1.1 copy-done.3
  39.5 1.4 copy-done.5
  40.9 7.2 %multiply_convert_fusion.2 = bf16[2,768,8,80]{1,3,2,0:T(8,128)(2,1)} fusion(bf16[8,80,2688]{2,1,0:T(8,128)(2,1)S(1)} %copy-done, bf16[2688,1,768]{2,0,1:T(8,128)(2,1)S(1)} %get-tuple-element.19, bf16[2688,1,768]{2,0,1:T(8,128)(2,1)S(1)} %get-tuple-element.18, f32[768,80]{0,1:T(8,128)S(1)} %get-tuple-element.17), kind=kOutput, calls=%fused_computation.27 | convolution fusion | flops 5303304192 | bytes 13910016 | tf_op jit(solution)/shard_map/fjx,xrs->rsfj/dot_general | solution.py:117
  48.1 3.6 %copy.41 = bf16[2,768,8,80]{3,2,1,0:T(8,128)(2,1)S(1)} copy(bf16[2,768,8,80]{1,3,2,0:T(8,128)(2,1)} %multiply_convert_fusion.2) | data formatting | bytes 3932160 | tf_op jit(solution)/shard_map/convert_element_type | solution.py:118
  51.7 0.6 fusion.54
  52.2 0.8 pad_maximum_fusion.3
  53.0 2.6 %copy.42 = bf16[32,8,6,8,80]{4,3,2,1,0:T(8,128)(2,1)} copy(bf16[32,8,6,8,80]{4,3,2,0,1:T(8,128)(2,1)S(1)} %pad_maximum_fusion.3) | data formatting | bytes 3932160 | tf_op jit(solution)/shard_map/concatenate
  55.6 11.5 %all-to-all-start = ((bf16[128,2,6,8,80]{4,3,2,1,0:T(8,128)(2,1)}), bf16[128,2,6,8,80]{4,3,2,1,0:T(8,128)(2,1)S(1)}, u32[]{:S(2)}, u32[]{:S(2)}) async-start(bf16[128,2,6,8,80]{4,3,2,1,0:T(8,128)(2,1)} %bitcast.87), calls=%async_computation | async-start | bytes 6291456 | tf_op jit(solution)/shard_map/all_to_all | solution.py:29
  67.1 0.1 dynamic_slice.3
  67.2 0.1 add_compare_fusion
  67.3 0.1 fusion.49
  67.4 1.0 divide_select_fusion
  68.3 40.5 %all-to-all-done = bf16[128,2,6,8,80]{4,3,2,1,0:T(8,128)(2,1)S(1)} async-done(((bf16[128,2,6,8,80]{4,3,2,1,0:T(8,128)(2,1)}), bf16[128,2,6,8,80]{4,3,2,1,0:T(8,128)(2,1)S(1)}, u32[]{:S(2)}, u32[]{:S(2)}) %all-to-all-start) | async-done | bytes 1966112 | tf_op jit(solution)/shard_map/all_to_all | solution.py:29
  108.8 5.3 %copy.43 = bf16[4,2,6,8,32,80]{5,4,3,2,1,0:T(8,128)(2,1)} copy(bf16[4,2,6,8,32,80]{5,3,2,1,0,4:T(8,128)(2,1)S(1)} %bitcast.86) | data formatting | bytes 3932160 | tf_op jit(solution)/shard_map/transpose | solution.py:18
  114.1 5.8 %reshape.237 = bf16[4,2,6,8,2560]{4,3,2,1,0:T(8,128)(2,1)S(1)} reshape(bf16[4,2,6,8,32,80]{5,4,3,2,1,0:T(8,128)(2,1)} %copy.43) | data formatting | bytes 3932160 | tf_op jit(solution)/shard_map/reshape | solution.py:20
  120.0 0.0 copy-start.10
  120.0 0.2 copy_bitcast_fusion.1
  120.2 1.3 copy-done.2
  121.5 0.1 slice.63
  121.6 1.4 rev.7
  123.0 1.7 fusion.30
  124.7 3.7 %fusion.36 = f32[2,6,32,384]{3,2,0,1:T(8,128)S(1)} fusion(bf16[6,1280,768]{2,1,0:T(8,128)(2,1)} %param.7, bf16[2,6,32,1280]{3,2,1,0:T(8,128)(2,1)S(1)} %get-tuple-element.14), kind=kOutput, calls=%fused_computation.45 | convolution fusion | flops 377487360 | bytes 7471104 | tf_op jit(solution)/shard_map/rsfj,sjq->rsfq/dot_general | solution.py:56
  128.3 0.0 copy-start.8
  128.4 3.7 %fusion.33 = f32[2,6,32,384]{3,2,0,1:T(8,128)S(1)} fusion(bf16[6,1280,768]{2,1,0:T(8,128)(2,1)} %param.7, bf16[2,6,32,1280]{3,2,1,0:T(8,128)(2,1)S(1)} %get-tuple-element.15), kind=kOutput, calls=%fused_computation.44 | convolution fusion | flops 377487360 | bytes 7471104 | tf_op jit(solution)/shard_map/rsfj,sjq->rsfq/dot_general | solution.py:59
  132.1 0.2 fusion.52
  132.3 1.9 copy.53
  134.2 4.5 %all-to-all-start.2 = ((f32[2,6,32,768]{3,0,1,2:T(2,128)}), f32[2,6,32,768]{3,0,1,2:T(2,128)}, u32[]{:S(2)}, u32[]{:S(2)}) async-start(f32[2,6,32,768]{3,0,1,2:T(2,128)} %copy.53), calls=%async_computation.2 | async-start | bytes 2359296 | tf_op jit(solution)/shard_map/all_to_all | solution.py:126
  138.7 4.6 %fusion.9 = f32[6,2,32,1280]{3,2,1,0:T(8,128)S(1)} fusion(bf16[6,1280,768]{2,1,0:T(8,128)(2,1)} %param.7, bf16[2,6,32,768]{3,2,0,1:T(8,128)(2,1)S(1)} %get-tuple-element.2), kind=kOutput, calls=%fused_computation.15 | convolution fusion | flops 377487360 | bytes 8159232 | tf_op jit(solution)/shard_map/rsfq,sjq->rsfj/dot_general | solution.py:70
  143.4 5.7 %fusion.39 = (bf16[2,6,32,1280]{3,2,0,1:T(8,128)(2,1)}, bf16[2,6,32,1280]{3,2,0,1:T(8,128)(2,1)S(1)}) fusion(f32[6,2,32,1280]{3,2,1,0:T(8,128)S(1)} %fusion.9, bf16[6,1280,768]{2,1,0:T(8,128)(2,1)} %param.7, bf16[2,6,32,768]{3,2,0,1:T(8,128)(2,1)} %copy-done.7), kind=kOutput, calls=%fused_computation.47 | convolution fusion | flops 379453440 | bytes 10125312 | tf_op jit(solution)/shard_map/rsfq,sjq->rsfj/dot_general | solution.py:76
  149.1 4.0 %rev.8 = bf16[2,6,32,1280]{3,2,0,1:T(8,128)(2,1)} reverse(bf16[2,6,32,1280]{3,2,0,1:T(8,128)(2,1)S(1)} %get-tuple-element.5), dimensions={3} | reverse | bytes 1966080 | tf_op jit(solution)/shard_map/jit(_flip)/rev | solution.py:100
  153.1 1.6 pad_maximum_fusion.5
  154.8 4.8 %reshape.239 = bf16[2,6,32,32,80]{4,3,2,0,1:T(8,128)(2,1)} reshape(bf16[2,6,32,2560]{3,2,0,1:T(8,128)(2,1)S(1)} %pad_maximum_fusion.5) | data formatting | bytes 3932160 | tf_op jit(solution)/shard_map/reshape | solution.py:13
  159.5 3.1 %copy.69 = bf16[2,6,32,32,80]{4,2,1,0,3:T(8,128)(2,1)S(1)} copy(bf16[2,6,32,32,80]{4,3,2,0,1:T(8,128)(2,1)} %reshape.239) | data formatting | bytes 3932160 | tf_op jit(solution)/shard_map/reshape | solution.py:13
  162.6 0.6 fusion.53
  163.2 2.1 pad_maximum_fusion.4
  165.3 5.7 %all-to-all-start.1 = ((bf16[128,2,6,8,80]{4,3,2,1,0:T(8,128)(2,1)}), bf16[128,2,6,8,80]{4,3,2,1,0:T(8,128)(2,1)S(1)}, u32[]{:S(2)}, u32[]{:S(2)}) async-start(bf16[128,2,6,8,80]{4,3,2,1,0:T(8,128)(2,1)} %bitcast.21), calls=%async_computation.1 | async-start | bytes 6291456 | tf_op jit(solution)/shard_map/all_to_all | solution.py:29
  171.1 1.1 copy.51
  172.1 2.5 %copy.54 = f32[2,4,6,8,768]{4,3,2,1,0:T(8,128)} copy(f32[2,4,6,8,768]{4,0,2,3,1:T(2,128)} %bitcast.33) | data formatting | bytes 2359296 | tf_op jit(solution)/shard_map/all_to_all | solution.py:126
  174.7 38.1 %all-to-all-done.1 = bf16[128,2,6,8,80]{4,3,2,1,0:T(8,128)(2,1)S(1)} async-done(((bf16[128,2,6,8,80]{4,3,2,1,0:T(8,128)(2,1)}), bf16[128,2,6,8,80]{4,3,2,1,0:T(8,128)(2,1)S(1)}, u32[]{:S(2)}, u32[]{:S(2)}) %all-to-all-start.1) | async-done | bytes 1966112 | tf_op jit(solution)/shard_map/all_to_all | solution.py:29
  212.7 0.9 copy.50
  213.7 0.6 broadcast_multiply_fusion
  214.3 0.7 copy-done.6
  214.9 1.5 copy-done.4
  216.4 12.1 %bitcast_multiply_fusion = f32[8,80,2688]{2,1,0:T(8,128)} fusion(bf16[2688,1,768]{2,0,1:T(8,128)(2,1)S(1)} %copy-done.6, bf16[2688,1,768]{2,0,1:T(8,128)(2,1)S(1)} %copy-done.4, bf16[2,768,8,80]{3,2,1,0:T(8,128)(2,1)S(1)} %broadcast_multiply_fusion), kind=kOutput, calls=%fused_computation.14 | convolution fusion | flops 5290672128 | bytes 17104896 | tf_op jit(solution)/shard_map/rsfj,xrs->fjx/dot_general | solution.py:132
  (19 shorter events, 0.0 us)
Async XLA Ops:
  0.6 40.2 %copy-start = (bf16[8,80,2688]{2,1,0:T(8,128)(2,1)S(1)}, bf16[8,80,2688]{2,1,0:T(8,128)(2,1)}, u32[]{:S(2)}) copy-start(bf16[8,80,2688]{2,1,0:T(8,128)(2,1)} %param.6) | copy-start | bytes 10321924
  0.6 36.8 %copy-start.9 = (s32[768]{0:T(1024)S(1)}, s32[768]{0:T(1024)}, u32[]{:S(2)}) copy-start(s32[768]{0:T(1024)} %param.8) | copy-start | bytes 9220
  0.7 36.8 %copy-start.11 = (s32[80]{0:T(128)S(1)}, s32[80]{0:T(128)}, u32[]{:S(2)}) copy-start(s32[80]{0:T(128)} %param.9) | copy-start | bytes 964
  37.5 2.0 copy-start.3
  37.5 3.4 %copy-start.5 = (bf16[2688,1,768]{2,0,1:T(8,128)(2,1)}, bf16[2688,1,768]{2,0,1:T(8,128)(2,1)S(1)}, u32[]{:S(2)}) copy-start(bf16[2688,1,768]{2,0,1:T(8,128)(2,1)S(1)} %get-tuple-element.19) | copy-start | bytes 12386308
  55.6 11.7 %copy-start.12 = (f32[32]{0:T(128)S(1)}, f32[32]{0:T(128)}, u32[]{:S(2)}) copy-start(f32[32]{0:T(128)} %param.11) | copy-start | bytes 388
  55.6 53.2 %all-to-all-start = ((bf16[128,2,6,8,80]{4,3,2,1,0:T(8,128)(2,1)}), bf16[128,2,6,8,80]{4,3,2,1,0:T(8,128)(2,1)S(1)}, u32[]{:S(2)}, u32[]{:S(2)}) async-start(bf16[128,2,6,8,80]{4,3,2,1,0:T(8,128)(2,1)} %bitcast.87), calls=%async_computation | async-start | bytes 6291456 | tf_op jit(solution)/shard_map/all_to_all | solution.py:29
  120.0 3.0 %copy-start.10 = (f32[1280]{0:T(1024)S(1)}, f32[1280]{0:T(1024)}, u32[]{:S(2)}) copy-start(f32[1280]{0:T(1024)} %param.10) | copy-start | bytes 15364
  120.2 1.3 copy-start.2
  128.3 3.7 %copy-start.8 = (f32[6,32,768]{2,1,0:T(8,128)S(1)}, f32[6,32,768]{2,1,0:T(8,128)}, u32[]{:S(2)}) copy-start(f32[6,32,768]{2,1,0:T(8,128)} %divide_select_fusion) | copy-start | bytes 1769476
  132.3 6.4 %copy-start.7 = (bf16[2,6,32,768]{3,2,0,1:T(8,128)(2,1)}, bf16[2,6,32,768]{3,2,0,1:T(8,128)(2,1)S(1)}, u32[]{:S(2)}) copy-start(bf16[2,6,32,768]{3,2,0,1:T(8,128)(2,1)S(1)} %get-tuple-element.2) | copy-start | bytes 1769476
  134.2 31.1 %all-to-all-start.2 = ((f32[2,6,32,768]{3,0,1,2:T(2,128)}), f32[2,6,32,768]{3,0,1,2:T(2,128)}, u32[]{:S(2)}, u32[]{:S(2)}) async-start(f32[2,6,32,768]{3,0,1,2:T(2,128)} %copy.53), calls=%async_computation.2 | async-start | bytes 2359296 | tf_op jit(solution)/shard_map/all_to_all | solution.py:126
  165.3 47.4 %all-to-all-start.1 = ((bf16[128,2,6,8,80]{4,3,2,1,0:T(8,128)(2,1)}), bf16[128,2,6,8,80]{4,3,2,1,0:T(8,128)(2,1)S(1)}, u32[]{:S(2)}, u32[]{:S(2)}) async-start(bf16[128,2,6,8,80]{4,3,2,1,0:T(8,128)(2,1)} %bitcast.21), calls=%async_computation.1 | async-start | bytes 6291456 | tf_op jit(solution)/shard_map/all_to_all | solution.py:29
  212.7 2.2 copy-start.6
  213.7 2.7 %copy-start.4 = (bf16[2688,1,768]{2,0,1:T(8,128)(2,1)S(1)}, bf16[2688,1,768]{2,0,1:T(8,128)(2,1)}, u32[]{:S(2)}) copy-start(bf16[2688,1,768]{2,0,1:T(8,128)(2,1)} %copy-done.3) | copy-start | bytes 12386308
  216.4 12.1 %copy-start.1 = (bf16[8,80,2688]{2,1,0:T(8,128)(2,1)S(1)}, bf16[8,80,2688]{2,1,0:T(8,128)(2,1)}, u32[]{:S(2)}) copy-start(bf16[8,80,2688]{2,1,0:T(8,128)(2,1)} %param.6) | copy-start | bytes 10321924
where the time goes:
time: 229 us; the launch traced here: 228 us
  waiting for transfers between devices  78.5 us (34%)
  other arithmetic  45.7 us (20%)
  local copies, waits for them, and re-layouts  44.6 us (19%)
  matrix products  37 us (16%)
  starting transfers between devices  21.7 us (9%)
    all_to_all x2, waiting for transfers between devices, exchange_both(): parts = lax.all_to_all(parts, axis, split_axis=0, concat_axis=0, tiled=True)  78.5 us
    another operation x2, other arithmetic  38.9 us
    all_to_all x2, starting transfers between devices, exchange_both(): parts = lax.all_to_all(parts, axis, split_axis=0, concat_axis=0, tiled=True)  17.2 us
    dot_general x1, matrix products, body(): jnp.einsum('rsfj,xrs->fjx', masked, angles, preferred_element_type=jnp.fl...  12.1 us
    reshape x2, local copies, waits for them, and re-layouts, split_up(): value.reshape(*shape[:dim], length, shape[dim] // length, *shape[dim + 1:])  7.89 us
    dot_general x1, matrix products, body(): jnp.einsum('fjx,xrs->rsfj', grid_in, angles, preferred_element_type=jnp.f...  7.19 us
    reshape x2, local copies, waits for them, and re-layouts, laid_out(): parts.reshape(*shape[:dim], shape[dim] * shape[dim + 1], *shape[dim + 2:])  6.02 us
    unnamed x26, local copies, waits for them, and re-layouts  5.99 us
  transfers between devices with their start and end apart: 3, of which 2 were waited for; matrix products, arithmetic and copies ran while one was open for 14% of the time, Pallas kernels for 0%

commit v1 on v0

v1 whole, which is shorter than its diff:
```python
import functools
import math

import jax
import jax.numpy as jnp
from jax import lax
from jax.experimental import pallas as pl
from jax.experimental.pallas import tpu as pltpu
from jax.sharding import PartitionSpec as P

LMAX = 1279
MESH = pl.DeviceIdType.MESH
F32 = jnp.float32
BF16 = jnp.bfloat16

LON = 2688
ROW_A, ROW_B, ROW_C = 14, 12, 16
GROUPS = 16
TRIG_ROWS = 48
NT = (((1,), (1,)), ((), ()))

ORDER = (
    (1, 1), (3, 3), (1, 3), (3, 1), (1, 0), (3, 0), (0, 1), (0, 3),
    (2, 1), (2, 3), (1, 2), (3, 2), (2, 0), (0, 2), (2, 2), (0, 0),
)


def position():
    lat = lax.axis_index("lat")
    return lat // 8, lax.rem(lat // 2, 4), lat, lax.axis_index("fld")


def group_at(step):
    z, x, _, _ = position()
    dz, dx = jnp.int32(0), jnp.int32(0)
    for n, (a, b) in enumerate(ORDER):
        dz = jnp.where(step == n, a, dz)
        dx = jnp.where(step == n, b, dx)
    return lax.rem(z + dz, 4) * 4 + lax.rem(x + dx, 4)


def greet():
    barrier = pltpu.get_barrier_semaphore()
    _, _, lat, fld = position()
    me = lat * 4 + fld

    def signal(n, carry):
        peer = lax.rem(me + n, 128)
        pl.semaphore_signal(
            barrier, inc=1, device_id=(peer // 4, lax.rem(peer, 4)), device_id_type=MESH
        )
        return carry

    lax.fori_loop(1, 128, signal, 0)


def greeted():
    pl.semaphore_wait(pltpu.get_barrier_semaphore(), 127)


def send_group(group, source, target, send_sem, recv_sem, own_sem):
    _, _, lat, fld = position()
    me = lat * 4 + fld

    def send(n, carry):
        to = group * 8 + n
        @pl.when(to != me)
        def _():
            pltpu.make_async_remote_copy(
                src_ref=source.at[to],
                dst_ref=target.at[me],
                send_sem=send_sem,
                recv_sem=recv_sem,
                device_id=(to // 4, lax.rem(to, 4)),
                device_id_type=MESH,
            ).start()

        @pl.when(to == me)
        def _():
            pltpu.make_async_copy(source.at[me], target.at[me], own_sem).start()

        return carry

    lax.fori_loop(0, 8, send, 0)


def wait_all(source, target, send_sem, recv_sem, own_sem):
    _, _, lat, fld = position()
    pltpu.make_async_copy(source.at[0], target.at[0], own_sem).wait()
    pltpu.make_async_remote_copy(
        src_ref=source.at[pl.ds(0, 127)],
        dst_ref=target.at[pl.ds(0, 127)],
        send_sem=send_sem,
        recv_sem=recv_sem,
        device_id=(lat, fld),
        device_id_type=MESH,
    ).wait()


def lanes(rows=16):
    return lax.broadcasted_iota(jnp.int32, (rows, 128), 1)


def swap_blocks(parts):
    block = lanes() // 16
    turned = [p if i == 0 else pltpu.roll(p, 16 * i, 1) for i, p in enumerate(parts)]
    row = [turned[(-i) % 8] for i in range(8)]
    for bit in (1, 2, 4):
        mask = (block & bit) != 0
        row = [jnp.where(mask, row[(i - bit) % 8], row[i]) for i in range(8)]
    return [p if d == 0 else pltpu.roll(p, 128 - 16 * d, 1) for d, p in enumerate(row)]


def make_table(trig_cos, trig_sin, group, half, uv, table):
    cos_b = trig_cos.at[group]
    sin_b = trig_sin.at[group]
    cos_c = cos_b[ROW_A + ROW_B : ROW_A + ROW_B + ROW_C]
    sin_c = sin_b[ROW_A + ROW_B : ROW_A + ROW_B + ROW_C]
    for b in range(ROW_B):
        cb, sb = cos_b[ROW_A + b : ROW_A + b + 1], sin_b[ROW_A + b : ROW_A + b + 1]
        uv[0, 16 * b : 16 * b + 16] = cb * cos_c - sb * sin_c
        uv[1, 16 * b : 16 * b + 16] = sb * cos_c + cb * sin_c
    for a in range(ROW_A):
        ca, sa = cos_b[a : a + 1], sin_b[a : a + 1]
        table[192 * a : 192 * a + 192, 128 * half : 128 * half + 128] = (
            ca * uv[0] - sa * uv[1]
        ).astype(BF16)


def forward_kernel(
    grid_ref, cos_ref, sin_ref, waves_ref, modes_ref, recv_ref, angles_ref,
    uv, table, result, last_rows, outbox, send_sem, recv_sem, own_sem, table_sem,
):
    greet()
    lane16 = lax.rem(lanes(), 16)

    def step_body(step, carry):
        groups = (group_at(2 * step), group_at(2 * step + 1))
        for half in range(2):
            make_table(cos_ref, sin_ref, groups[half], half, uv, table)
        copies = [
            pltpu.make_async_copy(
                table.at[:, pl.ds(128 * half, 128)],
                angles_ref.at[:, pl.ds(pl.multiple_of(groups[half] * 128, 128), 128)],
                table_sem.at[half],
            )
            for half in range(2)
        ]
        for copy in copies:
            copy.start()
        result[...] = jnp.dot(grid_ref[...], table[...], preferred_element_type=F32)
        for half in range(2):
            waves = waves_ref[groups[half]]
            for q in (4, 0, 1, 2, 3):
                keep = waves < modes_ref[16 * q : 16 * q + 16]
                parts = [
                    jnp.where(
                        keep,
                        result[80 * f + 16 * q : 80 * f + 16 * q + 16, 128 * half : 128 * half + 128],
                        0.0,
                    )
                    for f in range(8)
                ]
                for d, part in enumerate(swap_blocks(parts)):
                    if q == 4:
                        last_rows[d] = part
                        continue
                    if q < 3:
                        moved = pltpu.roll(last_rows[d], 12 - 4 * q, 1)
                        part = jnp.where(lane16 >= 12, moved, part)
                    outbox[groups[half] * 8 + d, 16 * q : 16 * q + 16] = part.astype(BF16)
        for copy in copies:
            copy.wait()

        @pl.when(step == 0)
        def _():
            greeted()

        for half in range(2):
            send_group(groups[half], outbox, recv_ref, send_sem, recv_sem, own_sem)
        return carry

    lax.fori_loop(0, GROUPS // 2, step_body, 0)
    wait_all(outbox, recv_ref, send_sem, recv_sem, own_sem)


def unpack_last(read):
    lane16 = lax.rem(lanes(), 16)
    last = jnp.zeros((16, 128), F32)
    for c in range(3):
        piece = pltpu.roll(read(c).astype(F32), 128 - (12 - 4 * c), 1)
        last = jnp.where((lane16 >= 4 * c) & (lane16 < 4 * c + 4), piece, last)
    return last


def flip_matrix():
    row = lax.broadcasted_iota(jnp.int32, (128, 128), 0)
    col = lax.broadcasted_iota(jnp.int32, (128, 128), 1)
    return jnp.where(row + col == 127, 1.0, 0.0).astype(BF16), jnp.where(
        row == col, 1.0, 0.0
    ).astype(BF16)


def project_kernel(
    waves_ref, inbox, table_ref, weight_ref, pick_ref, rate_ref, coeff_ref, folded, even, odd
):
    slot = pl.program_id(0)

    @pl.when(slot == 0)
    def _():
        def unpack(i, carry):
            for k in range(4):
                message = inbox.at[i * 4 + k]
                cols = slice(128 * k, 128 * k + 128)
                folded[pl.ds(pl.multiple_of(80 * i, 16), 64), cols] = message[...]
                last = unpack_last(lambda c: message[16 * c : 16 * c + 16])
                folded[pl.ds(pl.multiple_of(80 * i + 64, 16), 16), cols] = last.astype(BF16)
            return carry

        lax.fori_loop(0, 32, unpack, 0)
        flip, _ = flip_matrix()
        for b in range(10):
            north = folded[128 * b : 128 * b + 128].astype(F32)
            low = 1280 + 128 * (9 - b)
            south = jnp.dot(flip, folded[low : low + 128], preferred_element_type=F32)
            weight = weight_ref[128 * b : 128 * b + 128]
            for target, value in ((even, north + south), (odd, north - south)):
                part = (value * weight).astype(BF16)
                target[:, 128 * b : 128 * b + 128] = lax.dot_general(
                    pick_ref[...], part, NT, preferred_element_type=F32
                ).astype(BF16)

    rows = pl.ds(pl.multiple_of(64 * slot, 64), 64)
    table = table_ref.at[0]
    wave = waves_ref[slot]
    for parity, source in enumerate((even, odd)):
        cols = slice(384 * parity, 384 * parity + 384)
        raw = jnp.dot(source[rows], table[:, cols], preferred_element_type=F32)
        col = lax.broadcasted_iota(jnp.int32, (32, 384), 1)
        degree = wave + 2 * col + parity
        ratio = (degree * (degree + 1)).astype(F32) / float(LMAX * (LMAX + 1))
        square = ratio * ratio
        factor = 1.0 / (1.0 + rate_ref[...] * (square * square))
        factor = jnp.where(degree <= LMAX, factor, 0.0)
        coeff_ref[0, 0:32, cols] = (raw[0:32] * factor).astype(BF16)
        coeff_ref[0, 32:64, cols] = (raw[32:64] * factor).astype(BF16)


def expand_kernel(
    coeff_ref, table_ref, place_ref, recv_ref,
    north, south, wide, outbox, send_sem, recv_sem, own_sem,
):
    slot = pl.program_id(0)

    @pl.when(slot == 0)
    def _():
        greet()

    rows = pl.ds(pl.multiple_of(64 * slot, 64), 64)
    table = table_ref.at[0]
    sym = lax.dot_general(coeff_ref[0, :, 0:384], table[:, 0:384], NT, preferred_element_type=F32)
    anti = lax.dot_general(
        coeff_ref[0, :, 384:768], table[:, 384:768], NT, preferred_element_type=F32
    )
    north[rows] = (sym + anti).astype(BF16)
    south[rows] = (sym - anti).astype(BF16)

    @pl.when(slot == 5)
    def _():
        flip, same = flip_matrix()
        for b in range(10):
            cols = slice(128 * b, 128 * b + 128)
            for source, turn, low in (
                (north, same, 128 * b),
                (south, flip, 1280 + 128 * (9 - b)),
            ):
                placed = jnp.dot(
                    place_ref[...], source[:, cols], preferred_element_type=F32
                ).astype(BF16)
                wide[low : low + 128] = lax.dot_general(
                    turn, placed, NT, preferred_element_type=F32
                ).astype(BF16)
        lane16 = lax.rem(lanes(), 16)
        greeted()

        def pack(step, carry):
            group = group_at(step)
            for core in range(2):
                lat = group * 2 + core
                for k in range(4):
                    cols = slice(128 * k, 128 * k + 128)
                    to = lat * 4 + k
                    last = wide[pl.ds(pl.multiple_of(80 * lat + 64, 16), 16), cols].astype(F32)
                    for q in range(4):
                        part = wide[pl.ds(pl.multiple_of(80 * lat + 16 * q, 16), 16), cols]
                        if q < 3:
                            moved = pltpu.roll(last, 12 - 4 * q, 1)
                            part = jnp.where(lane16 >= 12, moved, part.astype(F32)).astype(BF16)
                        outbox[to, 16 * q : 16 * q + 16] = part
            send_group(group, outbox, recv_ref, send_sem, recv_sem, own_sem)
            return carry

        lax.fori_loop(0, GROUPS, pack, 0)
        wait_all(outbox, recv_ref, send_sem, recv_sem, own_sem)


def backward_kernel(inbox, angles_ref, waves_ref, modes_ref, out_ref, spread):
    @pl.when(pl.program_id(0) == 0)
    def _():
        for group in range(GROUPS):
            waves = waves_ref[group]
            for q in range(5):
                keep = waves < modes_ref[16 * q : 16 * q + 16]
                parts = []
                for d in range(8):
                    message = inbox.at[group * 8 + d]
                    if q < 4:
                        parts.append(message[16 * q : 16 * q + 16].astype(F32))
                    else:
                        parts.append(unpack_last(lambda c: message[16 * c : 16 * c + 16]))
                for f, part in enumerate(swap_blocks(parts)):
                    spread[80 * f + 16 * q : 80 * f + 16 * q + 16, 128 * group : 128 * group + 128] = (
                        jnp.where(keep, 2.0 * part, 0.0).astype(BF16)
                    )

    out_ref[...] = lax.dot_general(spread[...], angles_ref[...], NT, preferred_element_type=F32)


def trig_tables(wave_slot):
    waves = jnp.repeat(wave_slot.reshape(128, 6), 2, axis=1)
    waves = jnp.pad(waves, ((0, 0), (0, 4))).reshape(GROUPS, 1, 128)
    column = lax.broadcasted_iota(jnp.int32, (GROUPS, TRIG_ROWS, 128), 2) % 16
    row = lax.broadcasted_iota(jnp.int32, (GROUPS, TRIG_ROWS, 128), 1)
    first = row < ROW_A
    factor = jnp.where(
        first, 192 * row, jnp.where(row < ROW_A + ROW_B, 16 * (row - ROW_A), row - ROW_A - ROW_B)
    )
    turn = jnp.where(first & (column % 2 == 1), LON // 4, 0)
    index = (factor * waves + turn) % LON
    radians = index.astype(F32) * (2.0 * math.pi / LON)
    scale = jnp.where(first, jnp.where(column < 12, 1.0 / math.sqrt(LON), 0.0), 1.0)
    return jnp.cos(radians) * scale, jnp.sin(radians) * scale, waves


def pick_matrix():
    row = lax.broadcasted_iota(jnp.int32, (384, 512), 0)
    col = lax.broadcasted_iota(jnp.int32, (384, 512), 1)
    slot, part, block = row // 64, (row // 32) % 2, row % 32
    return jnp.where(col == 16 * block + 2 * slot + part, 1.0, 0.0).astype(BF16)


VMEM = pl.BlockSpec(memory_space=pltpu.VMEM)
SMEM = pl.BlockSpec(memory_space=pltpu.SMEM)
ANY = pl.BlockSpec(memory_space=pl.ANY)
INBOX = jax.ShapeDtypeStruct((128, 64, 128), BF16)
LIMIT = 60 * 1024 * 1024


def whole(shape):
    return pl.BlockSpec(shape, lambda i: (0,) * len(shape))


def body(grid_in, legendre, wave_slot, lat_modes, gauss_weight, diffusion):
    lat_index = lax.axis_index("lat")
    fld_index = lax.axis_index("fld")
    grid_rows = grid_in.reshape(640, LON)
    modes = lat_modes.reshape(80, 1)
    cosines, sines, waves = trig_tables(wave_slot)

    arrived, angles = pl.pallas_call(
        forward_kernel,
        name="forward",
        out_shape=(INBOX, jax.ShapeDtypeStruct((LON, 2048), BF16)),
        in_specs=[VMEM] * 5,
        out_specs=(ANY, ANY),
        scratch_shapes=[
            pltpu.VMEM((2, 192, 128), F32),
            pltpu.VMEM((LON, 256), BF16),
            pltpu.VMEM((640, 256), F32),
            pltpu.VMEM((8, 16, 128), F32),
            pltpu.VMEM((128, 64, 128), BF16),
            pltpu.SemaphoreType.DMA,
            pltpu.SemaphoreType.DMA,
            pltpu.SemaphoreType.DMA,
            pltpu.SemaphoreType.DMA((2,)),
        ],
        compiler_params=pltpu.CompilerParams(
            collective_id=0, has_side_effects=True, vmem_limit_bytes=LIMIT
        ),
    )(grid_rows, cosines, sines, waves, modes)

    own = lax.dynamic_slice_in_dim(wave_slot, (lat_index * 4 + fld_index) * 6, 6)
    table_spec = pl.BlockSpec((1, 1280, 768), lambda s: (s, 0, 0))
    coeff_spec = pl.BlockSpec((1, 64, 768), lambda s: (s, 0, 0))
    pick = pick_matrix()
    coeff = pl.pallas_call(
        project_kernel,
        name="project",
        grid=(6,),
        out_shape=jax.ShapeDtypeStruct((6, 64, 768), BF16),
        in_specs=[
            SMEM, whole((128, 64, 128)), table_spec, whole((1280, 1)), whole((384, 512)),
            whole((32, 1)),
        ],
        out_specs=coeff_spec,
        scratch_shapes=[
            pltpu.VMEM((2560, 512), BF16),
            pltpu.VMEM((384, 1280), BF16),
            pltpu.VMEM((384, 1280), BF16),
        ],
        compiler_params=pltpu.CompilerParams(vmem_limit_bytes=LIMIT),
        cost_estimate=pl.CostEstimate(
            flops=2 * 384 * 1280 * 768, bytes_accessed=14_000_000, transcendentals=0
        ),
    )(own, arrived, legendre, gauss_weight.reshape(1280, 1), pick, diffusion.reshape(32, 1))

    blocks = coeff.reshape(6, 2, 4, 8, 768)
    pieces = []
    for shift in range(4):
        piece = lax.dynamic_index_in_dim(blocks, (fld_index + shift) % 4, 2, keepdims=False)
        if shift:
            piece = lax.ppermute(piece, "fld", [(i, (i + shift) % 4) for i in range(4)])
        pieces.append(piece)

    returned = pl.pallas_call(
        expand_kernel,
        name="expand",
        grid=(6,),
        out_shape=INBOX,
        in_specs=[coeff_spec, table_spec, whole((512, 384))],
        out_specs=ANY,
        scratch_shapes=[
            pltpu.VMEM((384, 1280), BF16),
            pltpu.VMEM((384, 1280), BF16),
            pltpu.VMEM((2560, 512), BF16),
            pltpu.VMEM((128, 64, 128), BF16),
            pltpu.SemaphoreType.DMA,
            pltpu.SemaphoreType.DMA,
            pltpu.SemaphoreType.DMA,
        ],
        compiler_params=pltpu.CompilerParams(
            collective_id=1, has_side_effects=True, vmem_limit_bytes=LIMIT
        ),
        cost_estimate=pl.CostEstimate(
            flops=20 * 384 * 1280 * 768, bytes_accessed=14_000_000, transcendentals=0
        ),
    )(coeff, legendre, pick.T)

    grid_out = pl.pallas_call(
        backward_kernel,
        name="backward",
        grid=(7,),
        out_shape=jax.ShapeDtypeStruct((640, LON), F32),
        in_specs=[
            whole((128, 64, 128)),
            pl.BlockSpec((384, 2048), lambda i: (i, 0)),
            whole((GROUPS, 1, 128)),
            whole((80, 1)),
        ],
        out_specs=pl.BlockSpec((640, 384), lambda i: (0, i)),
        scratch_shapes=[pltpu.VMEM((640, 2048), BF16)],
        compiler_params=pltpu.CompilerParams(vmem_limit_bytes=LIMIT),
        cost_estimate=pl.CostEstimate(
            flops=2 * 640 * LON * 2048, bytes_accessed=20_000_000, transcendentals=0
        ),
    )(returned, angles, waves, modes)

    stacked = jnp.stack(pieces)
    spectra = jnp.stack(
        [
            lax.dynamic_index_in_dim(stacked, (fld_index - k) % 4, 0, keepdims=False)
            for k in range(4)
        ]
    )
    spectra = spectra.transpose(2, 0, 1, 3, 4).reshape(2, 24, 8, 768).astype(F32)
    return (grid_out.reshape(8, 80, LON), spectra)


def solution(mesh):
    return jax.shard_map(
        body,
        mesh=mesh,
        in_specs=(P("fld", "lat", None), P(("lat", "fld"), None, None), P(), P("lat"), P(), P()),
        out_specs=(P("fld", "lat", None), P(None, "lat", "fld", None)),
        check_vma=False,
    )
```

time: 229 us -> 145 us (0.63)
  Pallas kernels: 0 us -> 125 us
  waiting for transfers between devices: 78.5 us -> 0.01 us
  other arithmetic: 45.7 us -> 5.61 us
  matrix products: 37 us -> 0 us
  local copies, waits for them, and re-layouts: 44.6 us -> 9.85 us
  starting transfers between devices: 21.7 us -> 3.3 us
    pallas_call x0 -> x4, Pallas kernels: none -> 125 us  [the longest x1 44.6 us: body(): pl.pallas_call(expand_kernel, name='expand', grid=(6,), out_shape=INBOX,...]
    all_to_all x3 -> x0, waiting for transfers between devices: 78.5 us -> none  [the longest x2 78.5 us: exchange_both(): parts = lax.all_to_all(parts, axis, split_axis=0, concat_axis=0, tiled=True)]
    another operation x2 -> x1, other arithmetic: 38.9 us -> 0.08 us  [body(): stacked = jnp.stack(pieces)]
    dot_general x6 -> x0, matrix products: 37 us -> none  [the longest x1 12.1 us: body(): jnp.einsum('rsfj,xrs->fjx', masked, angles, preferred_element_type=jnp.fl...]
    all_to_all x3 -> x0, starting transfers between devices: 21.7 us -> none  [the longest x2 17.2 us: exchange_both(): parts = lax.all_to_all(parts, axis, split_axis=0, concat_axis=0, tiled=True)]
    reshape x4 -> x7, local copies, waits for them, and re-layouts: 13.9 us -> 6.03 us  [the longest x1 1.77 us: body(): gauss_weight.reshape(1280, 1)]
    transpose x2 -> x0, local copies, waits for them, and re-layouts: 6.27 us -> none  [the longest x1 5.34 us: laid_out(): parts = jnp.moveaxis(parts, 0, dim)]
    rev x2 -> x0, local copies, waits for them, and re-layouts: 5.41 us -> none  [the longest x1 4.03 us: transform_block(): jnp.flip((sym_part - anti_part).astype(jnp.bfloat16), -1)]
  transfers between devices with their start and end apart: 3 -> 3, of which waited for: 2 -> 0; matrix products, arithmetic and copies ran while one was open for 14% -> 1% of each run, Pallas kernels for 0% -> 47%
where the time goes in v1:
time: 145 us
  Pallas kernels  125 us (86%)
  local copies, waits for them, and re-layouts  9.85 us (7%)
  other arithmetic  5.61 us (4%)
  starting transfers between devices  3.3 us (2%)
    pallas_call x1, Pallas kernels, body(): pl.pallas_call(expand_kernel, name='expand', grid=(6,), out_shape=INBOX,...  44.6 us
    pallas_call x1, Pallas kernels, body(): pl.pallas_call(forward_kernel, name='forward', out_shape=(INBOX, jax.Shap...  42.5 us
    pallas_call x1, Pallas kernels, body(): pl.pallas_call(backward_kernel, name='backward', grid=(7,), out_shape=jax...  22.7 us
    pallas_call x1, Pallas kernels, body(): pl.pallas_call(project_kernel, name='project', grid=(6,), out_shape=jax.S...  15.1 us
    ppermute x3, starting transfers between devices, body(): piece = lax.ppermute(piece, 'fld', [(i, (i + shift) % 4) for i in range(4)])  3.3 us
  transfers between devices with their start and end apart: 3, of which 0 were waited for; matrix products, arithmetic and copies ran while one was open for 1% of the time, Pallas kernels for 47%

profile of v1, /device:TPU:1, one launch (start us, length us, event | category | flops | bytes accessed | tf_op | source)
XLA Modules:
  0.0 144.5 jit_solution(2361228748848341791)
XLA Ops:
  0.7 0.8 reshape.37
  1.5 0.1 copy.11
  1.6 0.1 copy.29
  1.7 0.1 mul.70
  1.8 0.7 reshape.39
  2.6 1.3 dynamic_slice.29.waves_ref
  3.9 1.4 copy.15.modes_ref
  5.3 1.8 %reshape.46.weight_ref = f32[1280,1]{1,0:T(8,128)} reshape(f32[1280]{0:T(1024)} %param.10) | data formatting | bytes 10240 | tf_op jit(solution)/shard_map/reshape | solution.py:415
  7.0 1.3 copy.17.rate_ref
  8.4 2.7 %sine_multiply_fusion = (f32[16,48,128]{2,1,0:T(8,128)}, f32[16,48,128]{2,1,0:T(8,128)}) fusion(s32[128]{0:T(128)S(1)} %get-tuple-element.24, s32[128]{0:T(128)S(1)} %get-tuple-element.25, pred[48]{0:T(512)(128)(4,1)S(1)} %get-tuple-element.23, pred[128]{0:T(512)(128)(4,1)S(1)} %compare_and_fusion, s32[16,128]{1,0:T(8,128)S(1)} %mul.70, ...), kind=kLoop, calls=%fused_computation.31 | loop fusion | flops 3145728 | bytes 796448 | tf_op jit(solution)/shard_map/mul | solution.py:342
  11.1 42.5 %forward.1 = (bf16[128,64,128]{2,1,0:T(8,128)(2,1)}, bf16[2688,2048]{1,0:T(8,128)(2,1)}) custom-call(bf16[640,2688]{1,0:T(8,128)(2,1)} %bitcast.31, f32[16,48,128]{2,1,0:T(8,128)} %get-tuple-element.17.cos_ref, f32[16,48,128]{2,1,0:T(8,128)} %get-tuple-element.16.sin_ref, s32[16,1,128]{2,1,0:T(1,128)} %bitcast.36, s32[80,1]{1,0:T(8,128)} %copy.15.modes_ref), custom_call_target="tpu_custom_call" | custom-call | tf_op jit(solution)/shard_map/forward/pallas_call | solution.py:370
  53.6 1.8 %select_convert_fusion.1.pick_ref = bf16[384,512]{1,0:T(8,128)(2,1)} fusion(s32[384]{0:T(512)S(1)} %get-tuple-element.26, s32[384]{0:T(512)S(1)} %get-tuple-element.30, s32[384]{0:T(512)S(1)} %get-tuple-element.27, s32[384]{0:T(512)S(1)} %get-tuple-element.31, s32[384]{0:T(512)S(1)} %get-tuple-element.28, s32[384]{0:T(512)S(1)} %get-tuple-element.29, ...), kind=kLoop, calls=%fused_computation.21 | loop fusion | flops 4128768 | bytes 403584 | tf_op jit(solution)/shard_map/convert_element_type | solution.py:349
  55.4 15.1 %project.1.coeff_ref = bf16[6,64,768]{2,1,0:T(8,128)(2,1)} custom-call(s32[6]{0:T(128)} %dynamic_slice.29.waves_ref, bf16[128,64,128]{2,1,0:T(8,128)(2,1)} %get-tuple-element.4.inbox, bf16[6,1280,768]{2,1,0:T(8,128)(2,1)} %table_ref.3, f32[1280,1]{1,0:T(8,128)} %reshape.46.weight_ref, bf16[384,512]{1,0:T(8,128)(2,1)} %select_convert_fusion.1.pick_ref, ...), custom_call_target="tpu_custom_call" | custom-call | flops 754974720 | bytes 14000000 | tf_op jit(solution)/shard_map/project/pallas_call | solution.py:396
  70.6 1.2 dynamic-slice_bitcast_fusion.3
  71.7 2.6 %collective-permute-start.2 = (bf16[6,2,8,768]{3,2,1,0:T(8,128)(2,1)S(1)}, bf16[6,2,8,768]{3,2,1,0:T(8,128)(2,1)S(1)}, u32[]{:S(2)}, u32[]{:S(2)}) collective-permute-start(bf16[6,2,8,768]{3,2,1,0:T(8,128)(2,1)S(1)} %get-tuple-element.15), channel_id=1, source_target_pairs={{0,3},{1,0},{2,1},{3,2},{4,7},{5,4},{6,5},{7,6},{8,11},{9,8},{10,9... | collective-permute-start | bytes 442376 | tf_op jit(solution)/shard_map/ppermute | solution.py:422
  74.4 0.0 collective-permute-start.1
  74.4 0.7 collective-permute-start
  75.0 0.9 select_convert_fusion.place_ref
  75.9 44.6 %expand.1.inbox = bf16[128,64,128]{2,1,0:T(8,128)(2,1)} custom-call(bf16[6,64,768]{2,1,0:T(8,128)(2,1)} %project.1.coeff_ref, bf16[6,1280,768]{2,1,0:T(8,128)(2,1)} %table_ref.3, bf16[512,384]{1,0:T(8,128)(2,1)} %select_convert_fusion.place_ref), custom_call_target="tpu_custom_call" | custom-call | flops 7549747200 | bytes 14000000 | tf_op jit(solution)/shard_map/expand/pallas_call | solution.py:425
  120.5 22.7 %backward.1 = f32[640,2688]{1,0:T(8,128)} custom-call(bf16[128,64,128]{2,1,0:T(8,128)(2,1)} %expand.1.inbox, bf16[2688,2048]{1,0:T(8,128)(2,1)} %get-tuple-element.5.angles_ref, s32[16,1,128]{2,1,0:T(1,128)} %bitcast.37, s32[80,1]{1,0:T(8,128)} %copy.15.modes_ref), custom_call_target="tpu_custom_call" | custom-call | flops 7046430720 | bytes 20000000 | tf_op jit(solution)/shard_map/backward/pallas_call | solution.py:449
  143.2 0.0 collective-permute-done.2
  143.2 0.0 collective-permute-done.1
  143.2 0.0 collective-permute-done
  143.2 0.1 pad_maximum_fusion
  143.3 0.1 constant_dynamic-slice_fusion.3
  143.3 0.1 maximum_convert_fusion
  143.4 1.1 copy.24
  (13 shorter events, 0.1 us)
Async XLA Ops:
  71.7 71.4 %collective-permute-start.2 = (bf16[6,2,8,768]{3,2,1,0:T(8,128)(2,1)S(1)}, bf16[6,2,8,768]{3,2,1,0:T(8,128)(2,1)S(1)}, u32[]{:S(2)}, u32[]{:S(2)}) collective-permute-start(bf16[6,2,8,768]{3,2,1,0:T(8,128)(2,1)S(1)} %get-tuple-element.15), channel_id=1, source_target_pairs={{0,3},{1,0},{2,1},{3,2},{4,7},{5,4},{6,5},{7,6},{8,11},{9,8},{10,9... | collective-permute-start | bytes 442376 | tf_op jit(solution)/shard_map/ppermute | solution.py:422
  74.4 68.8 %collective-permute-start.1 = (bf16[6,2,8,768]{3,2,1,0:T(8,128)(2,1)S(1)}, bf16[6,2,8,768]{3,2,1,0:T(8,128)(2,1)S(1)}, u32[]{:S(2)}, u32[]{:S(2)}) collective-permute-start(bf16[6,2,8,768]{3,2,1,0:T(8,128)(2,1)S(1)} %get-tuple-element.13), channel_id=1, source_target_pairs={{0,2},{1,3},{2,0},{3,1},{4,6},{5,7},{6,4},{7,5},{8,10},{9,11},{10,... | collective-permute-start | bytes 442376 | tf_op jit(solution)/shard_map/ppermute | solution.py:422
  74.4 68.8 %collective-permute-start = (bf16[6,2,8,768]{3,2,1,0:T(8,128)(2,1)S(1)}, bf16[6,2,8,768]{3,2,1,0:T(8,128)(2,1)S(1)}, u32[]{:S(2)}, u32[]{:S(2)}) collective-permute-start(bf16[6,2,8,768]{3,2,1,0:T(8,128)(2,1)S(1)} %get-tuple-element.14), channel_id=1, source_target_pairs={{0,1},{1,2},{2,3},{3,0},{4,5},{5,6},{6,7},{7,4},{8,9},{9,10},{10,1... | collective-permute-start | bytes 442376 | tf_op jit(solution)/shard_map/ppermute | solution.py:422

commit v2 on v1

v2 whole, which is shorter than its diff:
```python
import functools
import math

import jax
import jax.numpy as jnp
from jax import lax
from jax.experimental import pallas as pl
from jax.experimental.pallas import tpu as pltpu
from jax.sharding import PartitionSpec as P

LMAX = 1279
MESH = pl.DeviceIdType.MESH
F32 = jnp.float32
BF16 = jnp.bfloat16

LON = 2688
ROW_A, ROW_B, ROW_C = 14, 12, 16
GROUPS = 16
TRIG_ROWS = 48
NT = (((1,), (1,)), ((), ()))

ORDER = (
    (1, 1), (3, 3), (1, 3), (3, 1), (1, 0), (3, 0), (0, 1), (0, 3),
    (2, 1), (2, 3), (1, 2), (3, 2), (2, 0), (0, 2), (2, 2), (0, 0),
)


def position():
    lat = lax.axis_index("lat")
    return lat // 8, lax.rem(lat // 2, 4), lat, lax.axis_index("fld")


def group_at(step):
    z, x, _, _ = position()
    dz, dx = jnp.int32(0), jnp.int32(0)
    for n, (a, b) in enumerate(ORDER):
        dz = jnp.where(step == n, a, dz)
        dx = jnp.where(step == n, b, dx)
    return lax.rem(z + dz, 4) * 4 + lax.rem(x + dx, 4)


def greet():
    barrier = pltpu.get_barrier_semaphore()
    _, _, lat, fld = position()
    me = lat * 4 + fld

    def signal(n, carry):
        peer = lax.rem(me + n, 128)
        pl.semaphore_signal(
            barrier, inc=1, device_id=(peer // 4, lax.rem(peer, 4)), device_id_type=MESH
        )
        return carry

    lax.fori_loop(1, 128, signal, 0)


def greeted():
    pl.semaphore_wait(pltpu.get_barrier_semaphore(), 127)


def send_group(group, source, target, send_sem, recv_sem, own_sem):
    _, _, lat, fld = position()
    me = lat * 4 + fld

    def send(n, carry):
        to = group * 8 + n
        @pl.when(to != me)
        def _():
            pltpu.make_async_remote_copy(
                src_ref=source.at[to],
                dst_ref=target.at[me],
                send_sem=send_sem,
                recv_sem=recv_sem,
                device_id=(to // 4, lax.rem(to, 4)),
                device_id_type=MESH,
            ).start()

        @pl.when(to == me)
        def _():
            pltpu.make_async_copy(source.at[me], target.at[me], own_sem).start()

        return carry

    lax.fori_loop(0, 8, send, 0)


def wait_all(source, target, send_sem, recv_sem, own_sem):
    _, _, lat, fld = position()
    pltpu.make_async_copy(source.at[0], target.at[0], own_sem).wait()
    pltpu.make_async_remote_copy(
        src_ref=source.at[pl.ds(0, 127)],
        dst_ref=target.at[pl.ds(0, 127)],
        send_sem=send_sem,
        recv_sem=recv_sem,
        device_id=(lat, fld),
        device_id_type=MESH,
    ).wait()


def lanes(rows=16):
    return lax.broadcasted_iota(jnp.int32, (rows, 128), 1)


def aligned(start, size, unit=16):
    return pl.ds(pl.multiple_of(start, unit), size)


def swap_blocks(parts):
    block = lanes() // 16
    turned = [p if i == 0 else pltpu.roll(p, 16 * i, 1) for i, p in enumerate(parts)]
    row = [turned[(-i) % 8] for i in range(8)]
    for bit in (1, 2, 4):
        mask = (block & bit) != 0
        row = [jnp.where(mask, row[(i - bit) % 8], row[i]) for i in range(8)]
    return [p if d == 0 else pltpu.roll(p, 128 - 16 * d, 1) for d, p in enumerate(row)]


def spread_waves(slots_ref, waves):
    lane = lanes(GROUPS)
    group = lax.broadcasted_iota(jnp.int32, (GROUPS, 128), 0)
    flat = (8 * group + lane // 16) * 6 + jnp.minimum(lax.rem(lane, 16), 11) // 2
    at = lax.rem(flat, 128)
    total = jnp.zeros((GROUPS, 128), jnp.int32)
    for r in range(6):
        row = jnp.broadcast_to(slots_ref[r : r + 1], (GROUPS, 128))
        found = jnp.take_along_axis(row, at, axis=1, mode="promise_in_bounds")
        total = jnp.where(flat // 128 == r, found, total)
    waves[...] = total


def as_column(row):
    return jnp.broadcast_to(row, (128, 128)).T


def spread_modes(modes_ref, line, modes):
    line[...] = jnp.zeros((8, 128), F32)
    line[0:1, 0:80] = modes_ref[...].astype(F32)
    modes[...] = as_column(line[0:1])[0:80].astype(jnp.int32)


def fill_trig(waves, trig):
    column = lax.rem(lanes(TRIG_ROWS), 16)
    row = lax.broadcasted_iota(jnp.int32, (TRIG_ROWS, 128), 0)
    first = row < ROW_A
    factor = jnp.where(
        first, 192 * row, jnp.where(row < ROW_A + ROW_B, 16 * (row - ROW_A), row - ROW_A - ROW_B)
    )
    turn = jnp.where(first & (lax.rem(column, 2) == 1), LON // 4, 0)
    scale = jnp.where(first, jnp.where(column < 12, 1.0 / math.sqrt(LON), 0.0), 1.0)

    def one(group, carry):
        index = lax.rem(factor * waves[pl.ds(group, 1)] + turn, LON)
        radians = index.astype(F32) * (2.0 * math.pi / LON)
        trig[0, group] = jnp.cos(radians) * scale
        trig[1, group] = jnp.sin(radians) * scale
        return carry

    lax.fori_loop(0, GROUPS, one, 0)


def make_table(trig, group, half, uv, table):
    low = ROW_A + ROW_B
    cos_c = trig[0, group, low : low + ROW_C]
    sin_c = trig[1, group, low : low + ROW_C]
    for b in range(ROW_B):
        cb = trig[0, group, ROW_A + b : ROW_A + b + 1]
        sb = trig[1, group, ROW_A + b : ROW_A + b + 1]
        uv[0, 16 * b : 16 * b + 16] = cb * cos_c - sb * sin_c
        uv[1, 16 * b : 16 * b + 16] = sb * cos_c + cb * sin_c

    def rows(a, carry):
        ca, sa = trig[0, group, pl.ds(a, 1)], trig[1, group, pl.ds(a, 1)]
        table[aligned(192 * a, 192), 128 * half : 128 * half + 128] = (
            ca * uv[0] - sa * uv[1]
        ).astype(BF16)
        return carry

    lax.fori_loop(0, ROW_A, rows, 0)


def forward_kernel(
    grid_ref, slots_ref, modes_ref, recv_ref, angles_ref,
    waves, line, modes, trig, uv, table, result, last_rows, outbox,
    send_sem, recv_sem, own_sem, table_sem,
):
    greet()
    lane16 = lax.rem(lanes(), 16)
    spread_waves(slots_ref, waves)
    spread_modes(modes_ref, line, modes)
    fill_trig(waves, trig)

    def step_body(step, carry):
        groups = (group_at(2 * step), group_at(2 * step + 1))
        for half in range(2):
            make_table(trig, groups[half], half, uv, table)
        copies = [
            pltpu.make_async_copy(
                table.at[:, pl.ds(128 * half, 128)],
                angles_ref.at[:, aligned(groups[half] * 128, 128, 128)],
                table_sem.at[half],
            )
            for half in range(2)
        ]
        for copy in copies:
            copy.start()
        result[...] = jnp.dot(grid_ref[...], table[...], preferred_element_type=F32)
        for half in range(2):
            wave = waves[pl.ds(groups[half], 1)]

            def swapped(q):
                keep = wave < modes[aligned(16 * q, 16)]
                return swap_blocks([
                    jnp.where(
                        keep,
                        result[aligned(80 * f + 16 * q, 16), 128 * half : 128 * half + 128],
                        0.0,
                    )
                    for f in range(8)
                ])

            for d, part in enumerate(swapped(jnp.int32(4))):
                last_rows[d] = part

            def pack(q, carry):
                for d, part in enumerate(swapped(q)):
                    moved = pltpu.roll(last_rows[d], 12 - 4 * q, 1)
                    part = jnp.where((lane16 >= 12) & (q < 3), moved, part)
                    outbox[groups[half] * 8 + d, aligned(16 * q, 16)] = part.astype(BF16)
                return carry

            lax.fori_loop(0, 4, pack, 0)
        for copy in copies:
            copy.wait()

        @pl.when(step == 0)
        def _():
            greeted()

        for half in range(2):
            send_group(groups[half], outbox, recv_ref, send_sem, recv_sem, own_sem)
        return carry

    lax.fori_loop(0, GROUPS // 2, step_body, 0)
    wait_all(outbox, recv_ref, send_sem, recv_sem, own_sem)


def unpack_last(read):
    lane16 = lax.rem(lanes(), 16)
    last = jnp.zeros((16, 128), F32)
    for c in range(3):
        piece = pltpu.roll(read(c).astype(F32), 128 - (12 - 4 * c), 1)
        last = jnp.where((lane16 >= 4 * c) & (lane16 < 4 * c + 4), piece, last)
    return last


def turn_matrices():
    row = lax.broadcasted_iota(jnp.int32, (128, 128), 0)
    col = lax.broadcasted_iota(jnp.int32, (128, 128), 1)
    return jnp.where(row + col == 127, 1.0, 0.0).astype(BF16), jnp.where(
        row == col, 1.0, 0.0
    ).astype(BF16)


def fill_picks(pick, place):
    def rows_of(slot, carry):
        row = lax.broadcasted_iota(jnp.int32, (64, 512), 0)
        col = lax.broadcasted_iota(jnp.int32, (64, 512), 1)
        lane = 16 * lax.rem(row, 32) + row // 32 + 2 * slot
        pick[aligned(64 * slot, 64)] = jnp.where(col == lane, 1.0, 0.0).astype(BF16)
        return carry

    lax.fori_loop(0, 6, rows_of, 0)

    def lanes_of(block, carry):
        row = lax.broadcasted_iota(jnp.int32, (16, 384), 0)
        col = lax.broadcasted_iota(jnp.int32, (16, 384), 1)
        lane = (row // 2) * 64 + lax.rem(row, 2) * 32 + block
        place[aligned(16 * block, 16)] = jnp.where(
            (col == lane) & (row < 12), 1.0, 0.0
        ).astype(BF16)
        return carry

    lax.fori_loop(0, 32, lanes_of, 0)


def middle_kernel(
    slots_ref, inbox, table_ref, weight_ref, rate_ref, recv_ref, spec_ref,
    wide, even, odd, north, south, pick, place, line, rates, spec_box, outbox,
    send_sem, recv_sem, own_sem, spec_send, spec_recv, spec_own,
):
    slot = pl.program_id(0)
    _, _, lat, fld = position()

    @pl.when(slot == 0)
    def _():
        greet()
        fill_picks(pick, place)
        line[...] = jnp.zeros((8, 128), F32)
        line[0:1, 0:32] = rate_ref[...]
        rates[...] = as_column(line[0:1])[0:32]

        def unpack(i, carry):
            for k in range(4):
                message = inbox.at[i * 4 + k]
                cols = slice(128 * k, 128 * k + 128)
                wide[aligned(80 * i, 64), cols] = message[...]
                last = unpack_last(lambda c: message[16 * c : 16 * c + 16])
                wide[aligned(80 * i + 64, 16), cols] = last.astype(BF16)
            return carry

        lax.fori_loop(0, 32, unpack, 0)
        flip, _ = turn_matrices()

        def fold(b, carry):
            up = wide[aligned(128 * b, 128, 128)].astype(F32)
            low = wide[aligned(1280 + 128 * (9 - b), 128, 128)]
            down = jnp.dot(flip, low, preferred_element_type=F32)
            weight = as_column(weight_ref[pl.ds(b, 1)])[:, 0:1]
            for target, value in ((even, up + down), (odd, up - down)):
                part = (value * weight).astype(BF16)
                target[:, aligned(128 * b, 128, 128)] = lax.dot_general(
                    pick[...], part, NT, preferred_element_type=F32
                ).astype(BF16)
            return carry

        lax.fori_loop(0, 10, fold, 0)

    rows = aligned(64 * slot, 64)
    table = table_ref.at[0]
    wave = slots_ref[(lat * 4 + fld) * 6 + slot]
    sums = []
    for parity, source in enumerate((even, odd)):
        cols = slice(384 * parity, 384 * parity + 384)
        raw = jnp.dot(source[rows], table[:, cols], preferred_element_type=F32)
        col = lax.broadcasted_iota(jnp.int32, (32, 384), 1)
        degree = wave + 2 * col + parity
        ratio = (degree * (degree + 1)).astype(F32) / float(LMAX * (LMAX + 1))
        square = ratio * ratio
        factor = 1.0 / (1.0 + rates[:, 0:1] * (square * square))
        factor = jnp.where(degree <= LMAX, factor, 0.0)
        value = raw * jnp.concatenate([factor, factor], 0)
        for r in range(2):
            for k in range(4):
                spec_box[slot, r, k, :, cols] = value[32 * r + 8 * k : 32 * r + 8 * k + 8].astype(BF16)
        sums.append(
            lax.dot_general(value.astype(BF16), table[:, cols], NT, preferred_element_type=F32)
        )
    north[rows] = (sums[0] + sums[1]).astype(BF16)
    south[rows] = (sums[0] - sums[1]).astype(BF16)

    @pl.when(slot == 0)
    def _():
        greeted()

    for shift in range(4):
        to = lax.rem(fld + shift, 4)
        source, target = spec_box.at[slot, :, to], spec_ref.at[fld, slot]
        if shift:
            pltpu.make_async_remote_copy(
                src_ref=source, dst_ref=target, send_sem=spec_send, recv_sem=spec_recv,
                device_id=(lat, to), device_id_type=MESH,
            ).start()
        else:
            pltpu.make_async_copy(source, target, spec_own).start()

    @pl.when(slot == 5)
    def _():
        flip, same = turn_matrices()

        def turn(b, carry):
            cols = aligned(128 * b, 128, 128)
            for source, matrix, low in (
                (north, same, 128 * b),
                (south, flip, 1280 + 128 * (9 - b)),
            ):
                placed = jnp.dot(
                    place[...], source[:, cols], preferred_element_type=F32
                ).astype(BF16)
                wide[aligned(low, 128, 128)] = lax.dot_general(
                    matrix, placed, NT, preferred_element_type=F32
                ).astype(BF16)
            return carry

        lax.fori_loop(0, 10, turn, 0)
        lane16 = lax.rem(lanes(), 16)

        def pack(step, carry):
            group = group_at(step)
            for core in range(2):
                at = 80 * (group * 2 + core)
                for k in range(4):
                    cols = slice(128 * k, 128 * k + 128)
                    to = (group * 2 + core) * 4 + k
                    last = wide[aligned(at + 64, 16), cols].astype(F32)
                    for q in range(4):
                        part = wide[aligned(at + 16 * q, 16), cols]
                        if q < 3:
                            moved = pltpu.roll(last, 12 - 4 * q, 1)
                            part = jnp.where(lane16 >= 12, moved, part.astype(F32)).astype(BF16)
                        outbox[to, 16 * q : 16 * q + 16] = part
            send_group(group, outbox, recv_ref, send_sem, recv_sem, own_sem)
            return carry

        lax.fori_loop(0, GROUPS, pack, 0)
        pltpu.make_async_copy(spec_ref.at[0], spec_ref.at[0], spec_own).wait()
        pltpu.make_async_remote_copy(
            src_ref=spec_ref.at[pl.ds(0, 3)], dst_ref=spec_ref.at[pl.ds(0, 3)],
            send_sem=spec_send, recv_sem=spec_recv, device_id=(lat, fld), device_id_type=MESH,
        ).wait()
        wait_all(outbox, recv_ref, send_sem, recv_sem, own_sem)


def backward_kernel(inbox, angles_ref, slots_ref, modes_ref, out_ref, waves, line, modes, spread):
    @pl.when(pl.program_id(0) == 0)
    def _():
        spread_waves(slots_ref, waves)
        spread_modes(modes_ref, line, modes)

        def gather(group, carry):
            wave = waves[pl.ds(group, 1)]
            cols = aligned(128 * group, 128, 128)

            def put(q, parts):
                keep = wave < modes[aligned(16 * q, 16)]
                for f, part in enumerate(swap_blocks(parts)):
                    spread[aligned(80 * f + 16 * q, 16), cols] = jnp.where(
                        keep, 2.0 * part, 0.0
                    ).astype(BF16)

            def rows(q, carry):
                put(q, [inbox[group * 8 + d, aligned(16 * q, 16)].astype(F32) for d in range(8)])
                return carry

            lax.fori_loop(0, 4, rows, 0)
            put(
                jnp.int32(4),
                [
                    unpack_last(lambda c: inbox[group * 8 + d, 16 * c : 16 * c + 16])
                    for d in range(8)
                ],
            )
            return carry

        lax.fori_loop(0, GROUPS, gather, 0)

    out_ref[...] = lax.dot_general(spread[...], angles_ref[...], NT, preferred_element_type=F32)


VMEM = pl.BlockSpec(memory_space=pltpu.VMEM)
SMEM = pl.BlockSpec(memory_space=pltpu.SMEM)
ANY = pl.BlockSpec(memory_space=pl.ANY)
INBOX = jax.ShapeDtypeStruct((128, 64, 128), BF16)
LIMIT = 60 * 1024 * 1024


def whole(shape):
    return pl.BlockSpec(shape, lambda i: (0,) * len(shape))


def body(grid_in, legendre, wave_slot, lat_modes, gauss_weight, diffusion):
    grid_rows = grid_in.reshape(640, LON)
    modes = lat_modes.reshape(1, 80)
    slots = wave_slot.reshape(6, 128)

    arrived, angles = pl.pallas_call(
        forward_kernel,
        name="forward",
        out_shape=(INBOX, jax.ShapeDtypeStruct((LON, 2048), BF16)),
        in_specs=[VMEM] * 3,
        out_specs=(ANY, ANY),
        scratch_shapes=[
            pltpu.VMEM((GROUPS, 128), jnp.int32),
            pltpu.VMEM((8, 128), F32),
            pltpu.VMEM((80, 128), jnp.int32),
            pltpu.VMEM((2, GROUPS, TRIG_ROWS, 128), F32),
            pltpu.VMEM((2, 192, 128), F32),
            pltpu.VMEM((LON, 256), BF16),
            pltpu.VMEM((640, 256), F32),
            pltpu.VMEM((8, 16, 128), F32),
            pltpu.VMEM((128, 64, 128), BF16),
            pltpu.SemaphoreType.DMA,
            pltpu.SemaphoreType.DMA,
            pltpu.SemaphoreType.DMA,
            pltpu.SemaphoreType.DMA((2,)),
        ],
        compiler_params=pltpu.CompilerParams(
            collective_id=0, has_side_effects=True, vmem_limit_bytes=LIMIT
        ),
    )(grid_rows, slots, modes)

    returned, spectra = pl.pallas_call(
        middle_kernel,
        name="middle",
        grid=(6,),
        out_shape=(INBOX, jax.ShapeDtypeStruct((4, 6, 2, 8, 768), BF16)),
        in_specs=[
            SMEM,
            whole((128, 64, 128)),
            pl.BlockSpec((1, 1280, 768), lambda s: (s, 0, 0)),
            whole((10, 128)),
            whole((1, 32)),
        ],
        out_specs=(ANY, ANY),
        scratch_shapes=[
            pltpu.VMEM((2560, 512), BF16),
            pltpu.VMEM((384, 1280), BF16),
            pltpu.VMEM((384, 1280), BF16),
            pltpu.VMEM((384, 1280), BF16),
            pltpu.VMEM((384, 1280), BF16),
            pltpu.VMEM((384, 512), BF16),
            pltpu.VMEM((512, 384), BF16),
            pltpu.VMEM((8, 128), F32),
            pltpu.VMEM((32, 128), F32),
            pltpu.VMEM((6, 2, 4, 8, 768), BF16),
            pltpu.VMEM((128, 64, 128), BF16),
        ]
        + [pltpu.SemaphoreType.DMA] * 6,
        compiler_params=pltpu.CompilerParams(
            collective_id=1, has_side_effects=True, vmem_limit_bytes=LIMIT
        ),
    )(wave_slot, arrived, legendre, gauss_weight.reshape(10, 128), diffusion.reshape(1, 32))

    grid_out = pl.pallas_call(
        backward_kernel,
        name="backward",
        grid=(7,),
        out_shape=jax.ShapeDtypeStruct((640, LON), F32),
        in_specs=[
            whole((128, 64, 128)),
            pl.BlockSpec((384, 2048), lambda i: (i, 0)),
            whole((6, 128)),
            whole((1, 80)),
        ],
        out_specs=pl.BlockSpec((640, 384), lambda i: (0, i)),
        scratch_shapes=[
            pltpu.VMEM((GROUPS, 128), jnp.int32),
            pltpu.VMEM((8, 128), F32),
            pltpu.VMEM((80, 128), jnp.int32),
            pltpu.VMEM((640, 2048), BF16),
        ],
        compiler_params=pltpu.CompilerParams(vmem_limit_bytes=LIMIT),
    )(returned, angles, slots, modes)

    spectra = spectra.transpose(2, 0, 1, 3, 4).reshape(2, 24, 8, 768).astype(F32)
    return (grid_out.reshape(8, 80, LON), spectra)


def solution(mesh):
    return jax.shard_map(
        body,
        mesh=mesh,
        in_specs=(P("fld", "lat", None), P(("lat", "fld"), None, None), P(), P("lat"), P(), P()),
        out_specs=(P("fld", "lat", None), P(None, "lat", "fld", None)),
        check_vma=False,
    )
```

time: 145 us -> 138 us (0.952)
  Pallas kernels: 125 us -> 136 us
  local copies, waits for them, and re-layouts: 9.85 us -> 1.1 us
  other arithmetic: 5.61 us -> 0.12 us
  starting transfers between devices: 3.3 us -> 0 us
    pallas_call x1, Pallas kernels: 42.5 us -> 49.4 us  [body(): pl.pallas_call(forward_kernel, name='forward', out_shape=(INBOX, jax.Shap...]
    pallas_call x1, Pallas kernels: 22.7 us -> 29 us  [body(): pl.pallas_call(backward_kernel, name='backward', grid=(7,), out_shape=jax...]
    reshape x7 -> x0, local copies, waits for them, and re-layouts: 6.03 us -> none  [the longest x1 1.77 us: body(): gauss_weight.reshape(1280, 1)]
    ppermute x3 -> x0, starting transfers between devices: 3.3 us -> none  [body(): piece = lax.ppermute(piece, 'fld', [(i, (i + shift) % 4) for i in range(4)])]
    mul x2 -> x0, other arithmetic: 2.75 us -> none  [the longest x1 2.74 us: trig_tables(): return (jnp.cos(radians) * scale, jnp.sin(radians) * scale, waves)]
    convert_element_type x2 -> x0, other arithmetic: 2.64 us -> none  [pick_matrix(): return jnp.where(col == 16 * block + 2 * slot + part, 1.0, 0.0).astype(BF16)]
    pallas_call x2 -> x1, Pallas kernels: 59.7 us -> 57.4 us  [body(): pl.pallas_call(middle_kernel, name='middle', grid=(6,), out_shape=(INBOX,...]
  transfers between devices with their start and end apart: 3 -> 0, of which waited for: 0 -> 0; matrix products, arithmetic and copies ran while one was open for 1% -> 0% of each run, Pallas kernels for 47% -> 0%
where the time goes in v2:
time: 138 us
  Pallas kernels  136 us (99%)
    pallas_call x1, Pallas kernels, body(): pl.pallas_call(middle_kernel, name='middle', grid=(6,), out_shape=(INBOX,...  57.4 us
    pallas_call x1, Pallas kernels, body(): pl.pallas_call(forward_kernel, name='forward', out_shape=(INBOX, jax.Shap...  49.4 us
    pallas_call x1, Pallas kernels, body(): pl.pallas_call(backward_kernel, name='backward', grid=(7,), out_shape=jax...  29 us

profile of v2, /device:TPU:1, one launch (start us, length us, event | category | flops | bytes accessed | tf_op | source)
XLA Modules:
  0.0 137.6 jit_solution(13836217208458221446)
XLA Ops:
  0.6 49.4 %forward.1 = (bf16[128,64,128]{2,1,0:T(8,128)(2,1)}, bf16[2688,2048]{1,0:T(8,128)(2,1)}) custom-call(bf16[640,2688]{1,0:T(8,128)(2,1)} %bitcast.11, s32[6,128]{1,0:T(8,128)} %bitcast.12, s32[1,80]{1,0:T(1,128)} %bitcast.15), custom_call_target="tpu_custom_call" | custom-call | tf_op jit(solution)/shard_map/forward/pallas_call | solution.py:465
  50.0 57.4 %middle.1 = (bf16[128,64,128]{2,1,0:T(8,128)(2,1)}, bf16[4,6,2,8,768]{4,3,2,1,0:T(8,128)(2,1)}) custom-call(s32[768]{0:T(1024)} %slots_ref.1, bf16[128,64,128]{2,1,0:T(8,128)(2,1)} %get-tuple-element.6.inbox, bf16[6,1280,768]{2,1,0:T(8,128)(2,1)} %table_ref.1, f32[10,128]{1,0:T(8,128)} %bitcast.14, f32[1,32]{1,0:T(1,128)} %bitcast.17), custom_call_target="tpu_custom_call" | custom-call | tf_op jit(solution)/shard_map/middle/pallas_call | solution.py:491
  107.4 0.0 copy-start
  107.4 29.0 %backward.1 = f32[640,2688]{1,0:T(8,128)} custom-call(bf16[128,64,128]{2,1,0:T(8,128)(2,1)} %get-tuple-element.7.inbox, bf16[2688,2048]{1,0:T(8,128)(2,1)} %get-tuple-element.8.angles_ref, s32[6,128]{1,0:T(8,128)} %bitcast.13, s32[1,80]{1,0:T(1,128)} %bitcast.16), custom_call_target="tpu_custom_call" | custom-call | tf_op jit(solution)/shard_map/backward/pallas_call | solution.py:523
  136.4 0.0 copy-done
  136.4 0.1 convert_element_type.13
  136.5 1.1 copy.8
Async XLA Ops:
  107.4 29.0 %copy-start = (bf16[4,6,2,8,768]{4,3,2,1,0:T(8,128)(2,1)S(1)}, bf16[4,6,2,8,768]{4,3,2,1,0:T(8,128)(2,1)}, u32[]{:S(2)}) copy-start(bf16[4,6,2,8,768]{4,3,2,1,0:T(8,128)(2,1)} %get-tuple-element.9) | copy-start | bytes 1769476

commit v3 on v2

v3 whole, which is shorter than its diff:
```python
import functools
import math

import jax
import jax.numpy as jnp
from jax import lax
from jax.experimental import pallas as pl
from jax.experimental.pallas import tpu as pltpu
from jax.sharding import PartitionSpec as P

LMAX = 1279
MESH = pl.DeviceIdType.MESH
F32 = jnp.float32
BF16 = jnp.bfloat16

LON = 2688
ROW_A, ROW_B, ROW_C = 14, 12, 16
GROUPS = 16
TRIG_ROWS = 48
NT = (((1,), (1,)), ((), ()))

ORDER = (
    (1, 1), (3, 3), (1, 3), (3, 1), (1, 0), (3, 0), (0, 1), (0, 3),
    (2, 1), (2, 3), (1, 2), (3, 2), (2, 0), (0, 2), (2, 2), (0, 0),
)


def position():
    lat = lax.axis_index("lat")
    return lat // 8, lax.rem(lat // 2, 4), lat, lax.axis_index("fld")


def group_at(step):
    z, x, _, _ = position()
    dz, dx = jnp.int32(0), jnp.int32(0)
    for n, (a, b) in enumerate(ORDER):
        dz = jnp.where(step == n, a, dz)
        dx = jnp.where(step == n, b, dx)
    return lax.rem(z + dz, 4) * 4 + lax.rem(x + dx, 4)


def greet():
    barrier = pltpu.get_barrier_semaphore()
    _, _, lat, fld = position()
    me = lat * 4 + fld

    def signal(n, carry):
        peer = lax.rem(me + n, 128)
        pl.semaphore_signal(
            barrier, inc=1, device_id=(peer // 4, lax.rem(peer, 4)), device_id_type=MESH
        )
        return carry

    lax.fori_loop(1, 128, signal, 0)


def greeted():
    pl.semaphore_wait(pltpu.get_barrier_semaphore(), 127)


def send_one(to, source, target, send_sem, recv_sem, own_sem):
    _, _, lat, fld = position()
    me = lat * 4 + fld

    @pl.when(to != me)
    def _():
        pltpu.make_async_remote_copy(
            src_ref=source, dst_ref=target, send_sem=send_sem, recv_sem=recv_sem,
            device_id=(to // 4, lax.rem(to, 4)), device_id_type=MESH,
        ).start()

    @pl.when(to == me)
    def _():
        pltpu.make_async_copy(source, target, own_sem).start()


def wait_all(one, others, send_sem, recv_sem, own_sem):
    _, _, lat, fld = position()
    pltpu.make_async_copy(one, one, own_sem).wait()
    pltpu.make_async_remote_copy(
        src_ref=others, dst_ref=others, send_sem=send_sem, recv_sem=recv_sem,
        device_id=(lat, fld), device_id_type=MESH,
    ).wait()


def lanes(rows=16):
    return lax.broadcasted_iota(jnp.int32, (rows, 128), 1)


def aligned(start, size, unit=16):
    return pl.ds(pl.multiple_of(start, unit), size)


def swap_blocks(parts):
    block = lanes() // 16
    turned = [p if i == 0 else pltpu.roll(p, 16 * i, 1) for i, p in enumerate(parts)]
    row = [turned[(-i) % 8] for i in range(8)]
    for bit in (1, 2, 4):
        mask = (block & bit) != 0
        row = [jnp.where(mask, row[(i - bit) % 8], row[i]) for i in range(8)]
    return [p if d == 0 else pltpu.roll(p, 128 - 16 * d, 1) for d, p in enumerate(row)]


def spread_waves(slots_ref, waves):
    lane = lanes(GROUPS)
    group = lax.broadcasted_iota(jnp.int32, (GROUPS, 128), 0)
    flat = (8 * group + lane // 16) * 6 + jnp.minimum(lax.rem(lane, 16), 11) // 2
    at = lax.rem(flat, 128)
    total = jnp.zeros((GROUPS, 128), jnp.int32)
    for r in range(6):
        row = jnp.broadcast_to(slots_ref[r : r + 1], (GROUPS, 128))
        found = jnp.take_along_axis(row, at, axis=1, mode="promise_in_bounds")
        total = jnp.where(flat // 128 == r, found, total)
    waves[...] = total


def as_column(row):
    return jnp.broadcast_to(row, (128, 128)).T


def spread_modes(modes_ref, line, modes):
    line[...] = jnp.zeros((8, 128), F32)
    line[0:1, 0:80] = modes_ref[...].astype(F32)
    modes[...] = as_column(line[0:1])[0:80].astype(jnp.int32)


def fill_trig(waves, trig):
    column = lax.rem(lanes(TRIG_ROWS), 16)
    row = lax.broadcasted_iota(jnp.int32, (TRIG_ROWS, 128), 0)
    first = row < ROW_A
    factor = jnp.where(
        first, 192 * row, jnp.where(row < ROW_A + ROW_B, 16 * (row - ROW_A), row - ROW_A - ROW_B)
    )
    turn = jnp.where(first & (lax.rem(column, 2) == 1), LON // 4, 0)
    scale = jnp.where(first, jnp.where(column < 12, 1.0 / math.sqrt(LON), 0.0), 1.0)

    def one(group, carry):
        index = lax.rem(factor * waves[pl.ds(group, 1)] + turn, LON)
        radians = index.astype(F32) * (2.0 * math.pi / LON)
        trig[0, group] = jnp.cos(radians) * scale
        trig[1, group] = jnp.sin(radians) * scale
        return carry

    lax.fori_loop(0, GROUPS, one, 0)


def make_table(trig, group, half, uv, table):
    low = ROW_A + ROW_B
    cos_c = trig[0, group, low : low + ROW_C]
    sin_c = trig[1, group, low : low + ROW_C]
    for b in range(ROW_B):
        cb = trig[0, group, ROW_A + b : ROW_A + b + 1]
        sb = trig[1, group, ROW_A + b : ROW_A + b + 1]
        uv[0, 16 * b : 16 * b + 16] = cb * cos_c - sb * sin_c
        uv[1, 16 * b : 16 * b + 16] = sb * cos_c + cb * sin_c

    def rows(a, carry):
        ca, sa = trig[0, group, pl.ds(a, 1)], trig[1, group, pl.ds(a, 1)]
        table[aligned(192 * a, 192), 128 * half : 128 * half + 128] = (
            ca * uv[0] - sa * uv[1]
        ).astype(BF16)
        return carry

    lax.fori_loop(0, ROW_A, rows, 0)


def forward_kernel(
    grid_ref, slots_ref, modes_ref, recv_ref, angles_ref,
    waves, line, modes, trig, uv, table, result, outbox,
    send_sem, recv_sem, own_sem, table_sem,
):
    greet()
    lane16 = lax.rem(lanes(), 16)
    spread_waves(slots_ref, waves)
    spread_modes(modes_ref, line, modes)
    fill_trig(waves, trig)

    def step_body(step, carry):
        groups = (group_at(2 * step), group_at(2 * step + 1))
        for half in range(2):
            make_table(trig, groups[half], half, uv, table)
        copies = [
            pltpu.make_async_copy(
                table.at[:, pl.ds(128 * half, 128)],
                angles_ref.at[:, aligned(groups[half] * 128, 128, 128)],
                table_sem.at[half],
            )
            for half in range(2)
        ]
        for copy in copies:
            copy.start()
        result[...] = jnp.dot(grid_ref[...], table[...], preferred_element_type=F32)
        for half in range(2):
            wave = waves[pl.ds(groups[half], 1)]

            def swapped(q):
                keep = wave < modes[16 * q : 16 * q + 16]
                return swap_blocks([
                    jnp.where(
                        keep,
                        result[80 * f + 16 * q : 80 * f + 16 * q + 16, 128 * half : 128 * half + 128],
                        0.0,
                    )
                    for f in range(8)
                ])

            last = swapped(4)
            for q in range(4):
                for d, part in enumerate(swapped(q)):
                    if q < 3:
                        part = jnp.where(lane16 >= 12, pltpu.roll(last[d], 12 - 4 * q, 1), part)
                    outbox[groups[half] * 8 + d, 16 * q : 16 * q + 16] = part.astype(BF16)
        for copy in copies:
            copy.wait()

        @pl.when(step == 0)
        def _():
            greeted()

        _, _, lat, fld = position()
        landing = recv_ref.at[aligned(80 * lat, 64), aligned(128 * fld, 128, 128)]
        for half in range(2):
            def send(n, carry):
                to = groups[half] * 8 + n
                send_one(to, outbox.at[to], landing, send_sem, recv_sem, own_sem)
                return carry

            lax.fori_loop(0, 8, send, 0)
        return carry

    lax.fori_loop(0, GROUPS // 2, step_body, 0)
    wait_all(
        outbox.at[0], recv_ref.at[pl.ds(0, 2032)], send_sem, recv_sem, own_sem
    )


def unpack_last(read):
    lane16 = lax.rem(lanes(), 16)
    last = jnp.zeros((16, 128), F32)
    for c in range(3):
        piece = pltpu.roll(read(c).astype(F32), 128 - (12 - 4 * c), 1)
        last = jnp.where((lane16 >= 4 * c) & (lane16 < 4 * c + 4), piece, last)
    return last


def flip_matrix(size):
    row = lax.broadcasted_iota(jnp.int32, (size, size), 0)
    col = lax.broadcasted_iota(jnp.int32, (size, size), 1)
    return jnp.where(row + col == size - 1, 1.0, 0.0).astype(BF16)


def fill_picks(pick, place):
    def rows_of(slot, carry):
        row = lax.broadcasted_iota(jnp.int32, (64, 512), 0)
        col = lax.broadcasted_iota(jnp.int32, (64, 512), 1)
        lane = 16 * lax.rem(row, 32) + row // 32 + 2 * slot
        pick[aligned(64 * slot, 64)] = jnp.where(col == lane, 1.0, 0.0).astype(BF16)
        return carry

    lax.fori_loop(0, 6, rows_of, 0)

    def lanes_of(chunk, carry):
        row = lax.broadcasted_iota(jnp.int32, (64, 384), 0)
        col = lax.broadcasted_iota(jnp.int32, (64, 384), 1)
        block, inner = 4 * chunk + row // 16, lax.rem(row, 16)
        lane = (inner // 2) * 64 + lax.rem(inner, 2) * 32 + block
        place[aligned(64 * chunk, 64)] = jnp.where(
            (col == lane) & (inner < 12), 1.0, 0.0
        ).astype(BF16)
        return carry

    lax.fori_loop(0, 8, lanes_of, 0)


def middle_kernel(
    slots_ref, arrived_ref, tables_ref, weight_ref, rate_ref, recv_ref, spec_ref,
    wide, tables, even, odd, north, south, pick, place, line, rates, coeff, spec_box,
    send_sem, recv_sem, own_sem, spec_send, spec_recv, spec_own, wide_sem, table_sem,
):
    z, x, lat, fld = position()
    me = lat * 4 + fld
    load = pltpu.make_async_copy(arrived_ref, wide, wide_sem)
    load.start()
    table_loads = [
        pltpu.make_async_copy(tables_ref.at[s], tables.at[s], table_sem.at[s]) for s in range(6)
    ]
    for copy in table_loads:
        copy.start()
    greet()
    fill_picks(pick, place)
    line[...] = jnp.zeros((8, 128), F32)
    line[0:1, 0:32] = rate_ref[...]
    rates[...] = as_column(line[0:1])[0:32]
    load.wait()

    def unpack(n, carry):
        for i in range(2):
            at = 80 * (2 * n + i)
            for k in range(4):
                cols = slice(128 * k, 128 * k + 128)
                last = unpack_last(lambda c: wide[aligned(at + 16 * c, 16), cols])
                wide[aligned(at + 64, 16), cols] = last.astype(BF16)
        return carry

    lax.fori_loop(0, 16, unpack, 0)
    flip = flip_matrix(256)
    for b in range(5):
        up = wide[256 * b : 256 * b + 256].astype(F32)
        low = 1280 + 256 * (4 - b)
        down = jnp.dot(flip, wide[low : low + 256], preferred_element_type=F32)
        weight = jnp.concatenate(
            [as_column(weight_ref[2 * b + u : 2 * b + u + 1])[:, 0:1] for u in range(2)], 0
        )
        for target, value in ((even, up + down), (odd, up - down)):
            target[:, 256 * b : 256 * b + 256] = lax.dot_general(
                pick[...], (value * weight).astype(BF16), NT, preferred_element_type=F32
            ).astype(BF16)

    col = lax.broadcasted_iota(jnp.int32, (32, 384), 1)
    for slot in range(6):
        table_loads[slot].wait()
        wave = slots_ref[me * 6 + slot]
        for parity, source in enumerate((even, odd)):
            cols = slice(384 * parity, 384 * parity + 384)
            raw = jnp.dot(
                source[64 * slot : 64 * slot + 64], tables[slot, :, cols],
                preferred_element_type=F32,
            )
            degree = wave + 2 * col + parity
            ratio = (degree * (degree + 1)).astype(F32) / float(LMAX * (LMAX + 1))
            square = ratio * ratio
            factor = 1.0 / (1.0 + rates[:, 0:1] * (square * square))
            factor = jnp.where(degree <= LMAX, factor, 0.0)
            value = raw * jnp.concatenate([factor, factor], 0)
            for r in range(2):
                for k in range(4):
                    low = 32 * r + 8 * k
                    spec_box[slot, r, k, :, cols] = value[low : low + 8].astype(BF16)
            coeff[slot, :, cols] = value.astype(BF16)
        if slot == 0:
            greeted()
        for shift in range(4):
            to = lax.rem(fld + shift, 4)
            source, target = spec_box.at[slot, :, to], spec_ref.at[fld, slot]
            if shift:
                pltpu.make_async_remote_copy(
                    src_ref=source, dst_ref=target, send_sem=spec_send, recv_sem=spec_recv,
                    device_id=(lat, to), device_id_type=MESH,
                ).start()
            else:
                pltpu.make_async_copy(source, target, spec_own).start()

    turn = flip_matrix(320)
    lane16 = lax.rem(lanes(), 16)

    def part_of(step, carry):
        b = lax.rem(step + 2 * lax.rem(z, 2) + x // 2, 4)
        for slot in range(6):
            sums = [
                lax.dot_general(
                    tables[slot, aligned(320 * b, 320, 64), 384 * p : 384 * p + 384],
                    coeff[slot, :, 384 * p : 384 * p + 384],
                    NT,
                    preferred_element_type=F32,
                )
                for p in range(2)
            ]
            north[:, 64 * slot : 64 * slot + 64] = (sums[0] + sums[1]).astype(BF16)
            south[:, 64 * slot : 64 * slot + 64] = (sums[0] - sums[1]).astype(BF16)
        wide[aligned(320 * b, 320, 64)] = lax.dot_general(
            north[...], place[...], NT, preferred_element_type=F32
        ).astype(BF16)
        mirrored = jnp.dot(turn, south[...], preferred_element_type=F32).astype(BF16)
        wide[aligned(1280 + 320 * (3 - b), 320, 64)] = lax.dot_general(
            mirrored, place[...], NT, preferred_element_type=F32
        ).astype(BF16)

        def pack(n, carry):
            for i in (4 * b + n, 31 - 4 * b - n):
                at = 80 * i
                for k in range(4):
                    cols = slice(128 * k, 128 * k + 128)
                    last = wide[aligned(at + 64, 16), cols].astype(F32)
                    for q in range(3):
                        rows = aligned(at + 16 * q, 16)
                        moved = pltpu.roll(last, 12 - 4 * q, 1)
                        wide[rows, cols] = jnp.where(
                            lane16 >= 12, moved, wide[rows, cols].astype(F32)
                        ).astype(BF16)
            return carry

        lax.fori_loop(0, 4, pack, 0)

        def send(n, carry):
            for i in (4 * b + n, 31 - 4 * b - n):
                for k in range(4):
                    send_one(
                        i * 4 + k, wide.at[aligned(80 * i, 64), 128 * k : 128 * k + 128],
                        recv_ref.at[me], send_sem, recv_sem, own_sem,
                    )
            return carry

        lax.fori_loop(0, 4, send, 0)
        return carry

    lax.fori_loop(0, 4, part_of, 0)
    pltpu.make_async_copy(spec_ref.at[0], spec_ref.at[0], spec_own).wait()
    pltpu.make_async_remote_copy(
        src_ref=spec_ref.at[pl.ds(0, 3)], dst_ref=spec_ref.at[pl.ds(0, 3)],
        send_sem=spec_send, recv_sem=spec_recv, device_id=(lat, fld), device_id_type=MESH,
    ).wait()
    wait_all(recv_ref.at[0], recv_ref.at[pl.ds(0, 127)], send_sem, recv_sem, own_sem)


def backward_kernel(inbox, angles_ref, slots_ref, modes_ref, out_ref, waves, line, modes, spread):
    @pl.when(pl.program_id(0) == 0)
    def _():
        spread_waves(slots_ref, waves)
        spread_modes(modes_ref, line, modes)

        def gather(group, carry):
            wave = waves[pl.ds(group, 1)]
            cols = aligned(128 * group, 128, 128)

            for q in range(5):
                keep = wave < modes[16 * q : 16 * q + 16]
                if q < 4:
                    parts = [inbox[group * 8 + d, 16 * q : 16 * q + 16].astype(F32) for d in range(8)]
                else:
                    parts = [
                        unpack_last(lambda c: inbox[group * 8 + d, 16 * c : 16 * c + 16])
                        for d in range(8)
                    ]
                for f, part in enumerate(swap_blocks(parts)):
                    spread[80 * f + 16 * q : 80 * f + 16 * q + 16, cols] = jnp.where(
                        keep, 2.0 * part, 0.0
                    ).astype(BF16)
            return carry

        lax.fori_loop(0, GROUPS, gather, 0)

    out_ref[...] = lax.dot_general(spread[...], angles_ref[...], NT, preferred_element_type=F32)


VMEM = pl.BlockSpec(memory_space=pltpu.VMEM)
SMEM = pl.BlockSpec(memory_space=pltpu.SMEM)
ANY = pl.BlockSpec(memory_space=pl.ANY)
INBOX = jax.ShapeDtypeStruct((128, 64, 128), BF16)
LIMIT = 60 * 1024 * 1024


def whole(shape):
    return pl.BlockSpec(shape, lambda i: (0,) * len(shape))


def body(grid_in, legendre, wave_slot, lat_modes, gauss_weight, diffusion):
    grid_rows = grid_in.reshape(640, LON)
    modes = lat_modes.reshape(1, 80)
    slots = wave_slot.reshape(6, 128)

    arrived, angles = pl.pallas_call(
        forward_kernel,
        name="forward",
        out_shape=(
            jax.ShapeDtypeStruct((2560, 512), BF16),
            jax.ShapeDtypeStruct((LON, 2048), BF16),
        ),
        in_specs=[VMEM] * 3,
        out_specs=(ANY, ANY),
        scratch_shapes=[
            pltpu.VMEM((GROUPS, 128), jnp.int32),
            pltpu.VMEM((8, 128), F32),
            pltpu.VMEM((80, 128), jnp.int32),
            pltpu.VMEM((2, GROUPS, TRIG_ROWS, 128), F32),
            pltpu.VMEM((2, 192, 128), F32),
            pltpu.VMEM((LON, 256), BF16),
            pltpu.VMEM((640, 256), F32),
            pltpu.VMEM((128, 64, 128), BF16),
            pltpu.SemaphoreType.DMA,
            pltpu.SemaphoreType.DMA,
            pltpu.SemaphoreType.DMA,
            pltpu.SemaphoreType.DMA((2,)),
        ],
        compiler_params=pltpu.CompilerParams(
            collective_id=0, has_side_effects=True, vmem_limit_bytes=LIMIT
        ),
    )(grid_rows, slots, modes)

    returned, spectra = pl.pallas_call(
        middle_kernel,
        name="middle",
        out_shape=(INBOX, jax.ShapeDtypeStruct((4, 6, 2, 8, 768), BF16)),
        in_specs=[SMEM, ANY, ANY, VMEM, VMEM],
        out_specs=(ANY, ANY),
        scratch_shapes=[
            pltpu.VMEM((2560, 512), BF16),
            pltpu.VMEM((6, 1280, 768), BF16),
            pltpu.VMEM((384, 1280), BF16),
            pltpu.VMEM((384, 1280), BF16),
            pltpu.VMEM((320, 384), BF16),
            pltpu.VMEM((320, 384), BF16),
            pltpu.VMEM((384, 512), BF16),
            pltpu.VMEM((512, 384), BF16),
            pltpu.VMEM((8, 128), F32),
            pltpu.VMEM((32, 128), F32),
            pltpu.VMEM((6, 64, 768), BF16),
            pltpu.VMEM((6, 2, 4, 8, 768), BF16),
        ]
        + [pltpu.SemaphoreType.DMA] * 7
        + [pltpu.SemaphoreType.DMA((6,))],
        compiler_params=pltpu.CompilerParams(
            collective_id=1, has_side_effects=True, vmem_limit_bytes=LIMIT
        ),
    )(wave_slot, arrived, legendre, gauss_weight.reshape(10, 128), diffusion.reshape(1, 32))

    grid_out = pl.pallas_call(
        backward_kernel,
        name="backward",
        grid=(7,),
        out_shape=jax.ShapeDtypeStruct((640, LON), F32),
        in_specs=[
            whole((128, 64, 128)),
            pl.BlockSpec((384, 2048), lambda i: (i, 0)),
            whole((6, 128)),
            whole((1, 80)),
        ],
        out_specs=pl.BlockSpec((640, 384), lambda i: (0, i)),
        scratch_shapes=[
            pltpu.VMEM((GROUPS, 128), jnp.int32),
            pltpu.VMEM((8, 128), F32),
            pltpu.VMEM((80, 128), jnp.int32),
            pltpu.VMEM((640, 2048), BF16),
        ],
        compiler_params=pltpu.CompilerParams(vmem_limit_bytes=LIMIT),
    )(returned, angles, slots, modes)

    spectra = spectra.transpose(2, 0, 1, 3, 4).reshape(2, 24, 8, 768).astype(F32)
    return (grid_out.reshape(8, 80, LON), spectra)


def solution(mesh):
    return jax.shard_map(
        body,
        mesh=mesh,
        in_specs=(P("fld", "lat", None), P(("lat", "fld"), None, None), P(), P("lat"), P(), P()),
        out_specs=(P("fld", "lat", None), P(None, "lat", "fld", None)),
        check_vma=False,
    )
```

time: 138 us -> 121 us (0.88)
  Pallas kernels: 136 us -> 119 us
    pallas_call x1, Pallas kernels: 29 us -> 19.2 us  [body(): pl.pallas_call(backward_kernel, name='backward', grid=(7,), out_shape=jax...]
    pallas_call x2, Pallas kernels: 107 us -> 99.8 us  [the longest x1 54.7 us: body(): pl.pallas_call(middle_kernel, name='middle', out_shape=(INBOX, jax.ShapeD...]
where the time goes in v3:
time: 121 us
  Pallas kernels  119 us (98%)
    pallas_call x1, Pallas kernels, body(): pl.pallas_call(middle_kernel, name='middle', out_shape=(INBOX, jax.ShapeD...  54.7 us
    pallas_call x1, Pallas kernels, body(): pl.pallas_call(forward_kernel, name='forward', out_shape=(jax.ShapeDtypeS...  45 us
    pallas_call x1, Pallas kernels, body(): pl.pallas_call(backward_kernel, name='backward', grid=(7,), out_shape=jax...  19.2 us

profile of v3, /device:TPU:1, one launch (start us, length us, event | category | flops | bytes accessed | tf_op | source)
XLA Modules:
  0.0 120.8 jit_solution(7070130976245251659)
XLA Ops:
  0.6 45.0 %forward.1 = (bf16[2560,512]{1,0:T(8,128)(2,1)}, bf16[2688,2048]{1,0:T(8,128)(2,1)}) custom-call(bf16[640,2688]{1,0:T(8,128)(2,1)} %bitcast.11, s32[6,128]{1,0:T(8,128)} %bitcast.12, s32[1,80]{1,0:T(1,128)} %bitcast.15), custom_call_target="tpu_custom_call" | custom-call | tf_op jit(solution)/shard_map/forward/pallas_call | solution.py:461
  45.7 54.7 %middle.1 = (bf16[128,64,128]{2,1,0:T(8,128)(2,1)}, bf16[4,6,2,8,768]{4,3,2,1,0:T(8,128)(2,1)}) custom-call(s32[768]{0:T(1024)} %slots_ref.1, bf16[2560,512]{1,0:T(8,128)(2,1)} %get-tuple-element.6.arrived_ref, bf16[6,1280,768]{2,1,0:T(8,128)(2,1)} %tables_ref.1, f32[10,128]{1,0:T(8,128)} %bitcast.14, f32[1,32]{1,0:T(1,128)} %bitcast.17), custom_call_target="tpu_custom_call" | custom-call | tf_op jit(solution)/shard_map/middle/pallas_call | solution.py:489
  100.4 0.0 copy-start
  100.4 19.2 %backward.1 = f32[640,2688]{1,0:T(8,128)} custom-call(bf16[128,64,128]{2,1,0:T(8,128)(2,1)} %get-tuple-element.7.inbox, bf16[2688,2048]{1,0:T(8,128)(2,1)} %get-tuple-element.8.angles_ref, s32[6,128]{1,0:T(8,128)} %bitcast.13, s32[1,80]{1,0:T(1,128)} %bitcast.16), custom_call_target="tpu_custom_call" | custom-call | tf_op jit(solution)/shard_map/backward/pallas_call | solution.py:516
  119.6 0.0 copy-done
  119.6 0.1 convert_element_type.13
  119.7 1.1 copy.8
Async XLA Ops:
  100.4 19.2 %copy-start = (bf16[4,6,2,8,768]{4,3,2,1,0:T(8,128)(2,1)S(1)}, bf16[4,6,2,8,768]{4,3,2,1,0:T(8,128)(2,1)}, u32[]{:S(2)}) copy-start(bf16[4,6,2,8,768]{4,3,2,1,0:T(8,128)(2,1)} %get-tuple-element.9) | copy-start | bytes 1769476

commit v4 on v3

--- a/solution.py
+++ b/solution.py
@@ -20,8 +20,8 @@
 NT = (((1,), (1,)), ((), ()))
 
 ORDER = (
-    (1, 1), (3, 3), (1, 3), (3, 1), (1, 0), (3, 0), (0, 1), (0, 3),
-    (2, 1), (2, 3), (1, 2), (3, 2), (2, 0), (0, 2), (2, 2), (0, 0),
+    (1, 1), (3, 3), (1, 2), (3, 0), (2, 1), (0, 3), (1, 3), (3, 1),
+    (3, 2), (1, 0), (2, 3), (0, 1), (2, 0), (0, 2), (2, 2), (0, 0),
 )
 
 
@@ -294,15 +294,18 @@
     load.wait()
 
     def unpack(n, carry):
-        for i in range(2):
-            at = 80 * (2 * n + i)
+        done = []
+        for i in range(4):
+            at = 80 * (4 * n + i)
             for k in range(4):
                 cols = slice(128 * k, 128 * k + 128)
                 last = unpack_last(lambda c: wide[aligned(at + 16 * c, 16), cols])
-                wide[aligned(at + 64, 16), cols] = last.astype(BF16)
-        return carry
-
-    lax.fori_loop(0, 16, unpack, 0)
+                done.append((at, cols, last.astype(BF16)))
+        for at, cols, last in done:
+            wide[aligned(at + 64, 16), cols] = last
+        return carry
+
+    lax.fori_loop(0, 8, unpack, 0)
     flip = flip_matrix(256)
     for b in range(5):
         up = wide[256 * b : 256 * b + 256].astype(F32)
@@ -376,6 +379,7 @@
         ).astype(BF16)
 
         def pack(n, carry):
+            done = []
             for i in (4 * b + n, 31 - 4 * b - n):
                 at = 80 * i
                 for k in range(4):
@@ -384,9 +388,10 @@
                     for q in range(3):
                         rows = aligned(at + 16 * q, 16)
                         moved = pltpu.roll(last, 12 - 4 * q, 1)
-                        wide[rows, cols] = jnp.where(
-                            lane16 >= 12, moved, wide[rows, cols].astype(F32)
-                        ).astype(BF16)
+                        part = jnp.where(lane16 >= 12, moved, wide[rows, cols].astype(F32))
+                        done.append((rows, cols, part.astype(BF16)))
+            for rows, cols, part in done:
+                wide[rows, cols] = part
             return carry
 
         lax.fori_loop(0, 4, pack, 0)

time: 121 us -> 107 us (0.88)
  Pallas kernels: 119 us -> 104 us
    pallas_call x1, Pallas kernels: 54.7 us -> 42.5 us  [body(): pl.pallas_call(middle_kernel, name='middle', out_shape=(INBOX, jax.ShapeD...]
    pallas_call x1, Pallas kernels: 45 us -> 42.4 us  [body(): pl.pallas_call(forward_kernel, name='forward', out_shape=(jax.ShapeDtypeS...]
where the time goes in v4:
time: 107 us; the launch traced here: 106 us
  Pallas kernels  104 us (97%)
  local copies, waits for them, and re-layouts  1.1 us (1%)
    pallas_call x1, Pallas kernels, body(): pl.pallas_call(middle_kernel, name='middle', out_shape=(INBOX, jax.ShapeD...  42.5 us
    pallas_call x1, Pallas kernels, body(): pl.pallas_call(forward_kernel, name='forward', out_shape=(jax.ShapeDtypeS...  42.4 us
    pallas_call x1, Pallas kernels, body(): pl.pallas_call(backward_kernel, name='backward', grid=(7,), out_shape=jax...  19.2 us

profile of v4, /device:TPU:1, one launch (start us, length us, event | category | flops | bytes accessed | tf_op | source)
XLA Modules:
  0.0 106.0 jit_solution(14622821916233598407)
XLA Ops:
  0.6 42.4 %forward.1 = (bf16[2560,512]{1,0:T(8,128)(2,1)}, bf16[2688,2048]{1,0:T(8,128)(2,1)}) custom-call(bf16[640,2688]{1,0:T(8,128)(2,1)} %bitcast.11, s32[6,128]{1,0:T(8,128)} %bitcast.12, s32[1,80]{1,0:T(1,128)} %bitcast.15), custom_call_target="tpu_custom_call" | custom-call | tf_op jit(solution)/shard_map/forward/pallas_call | solution.py:466
  43.1 42.5 %middle.1 = (bf16[128,64,128]{2,1,0:T(8,128)(2,1)}, bf16[4,6,2,8,768]{4,3,2,1,0:T(8,128)(2,1)}) custom-call(s32[768]{0:T(1024)} %slots_ref.1, bf16[2560,512]{1,0:T(8,128)(2,1)} %get-tuple-element.6.arrived_ref, bf16[6,1280,768]{2,1,0:T(8,128)(2,1)} %tables_ref.1, f32[10,128]{1,0:T(8,128)} %bitcast.14, f32[1,32]{1,0:T(1,128)} %bitcast.17), custom_call_target="tpu_custom_call" | custom-call | tf_op jit(solution)/shard_map/middle/pallas_call | solution.py:494
  85.6 0.0 copy-start
  85.6 19.2 %backward.1 = f32[640,2688]{1,0:T(8,128)} custom-call(bf16[128,64,128]{2,1,0:T(8,128)(2,1)} %get-tuple-element.7.inbox, bf16[2688,2048]{1,0:T(8,128)(2,1)} %get-tuple-element.8.angles_ref, s32[6,128]{1,0:T(8,128)} %bitcast.13, s32[1,80]{1,0:T(1,128)} %bitcast.16), custom_call_target="tpu_custom_call" | custom-call | tf_op jit(solution)/shard_map/backward/pallas_call | solution.py:521
  104.7 0.0 copy-done
  104.7 0.1 convert_element_type.13
  104.9 1.1 %copy.8 = f32[2,24,8,768]{3,2,1,0:T(8,128)} copy(f32[2,24,8,768]{3,2,0,1:T(8,128)S(1)} %bitcast.10) | data formatting | bytes 2359296
Async XLA Ops:
  85.6 19.2 %copy-start = (bf16[4,6,2,8,768]{4,3,2,1,0:T(8,128)(2,1)S(1)}, bf16[4,6,2,8,768]{4,3,2,1,0:T(8,128)(2,1)}, u32[]{:S(2)}) copy-start(bf16[4,6,2,8,768]{4,3,2,1,0:T(8,128)(2,1)} %get-tuple-element.9) | copy-start | bytes 1769476

commit v5 on v4

--- a/solution.py
+++ b/solution.py
@@ -273,9 +273,12 @@
 
 
 def middle_kernel(
-    slots_ref, arrived_ref, tables_ref, weight_ref, rate_ref, recv_ref, spec_ref,
+    slots_ref, arrived_ref, tables_ref, weight_ref, rate_ref, rows_ref, modes_ref, angles_ref,
+    partial_ref, rest_ref, spec_ref,
     wide, tables, even, odd, north, south, pick, place, line, rates, coeff, spec_box,
-    send_sem, recv_sem, own_sem, spec_send, spec_recv, spec_own, wide_sem, table_sem,
+    waves, modes, angles, total, inbox, spread,
+    send_sem, own_sem, spec_send, spec_recv, spec_own, wide_sem, angle_sem, out_sem, rest_sem,
+    recv_sem, table_sem,
 ):
     z, x, lat, fld = position()
     me = lat * 4 + fld
@@ -291,6 +294,8 @@
     line[...] = jnp.zeros((8, 128), F32)
     line[0:1, 0:32] = rate_ref[...]
     rates[...] = as_column(line[0:1])[0:32]
+    spread_waves(rows_ref, waves)
+    spread_modes(modes_ref, line, modes)
     load.wait()
 
     def unpack(n, carry):
@@ -342,6 +347,9 @@
             coeff[slot, :, cols] = value.astype(BF16)
         if slot == 0:
             greeted()
+        if slot == 5:
+            angle_load = pltpu.make_async_copy(angles_ref, angles, angle_sem)
+            angle_load.start()
         for shift in range(4):
             to = lax.rem(fld + shift, 4)
             source, target = spec_box.at[slot, :, to], spec_ref.at[fld, slot]
@@ -353,11 +361,12 @@
             else:
                 pltpu.make_async_copy(source, target, spec_own).start()
 
+    mine = 2 * lax.rem(z, 2) + x // 2
     turn = flip_matrix(320)
     lane16 = lax.rem(lanes(), 16)
 
     def part_of(step, carry):
-        b = lax.rem(step + 2 * lax.rem(z, 2) + x // 2, 4)
+        b = lax.rem(step + mine, 4)
         for slot in range(6):
             sums = [
                 lax.dot_general(
@@ -401,7 +410,7 @@
                 for k in range(4):
                     send_one(
                         i * 4 + k, wide.at[aligned(80 * i, 64), 128 * k : 128 * k + 128],
-                        recv_ref.at[me], send_sem, recv_sem, own_sem,
+                        inbox.at[me], send_sem, recv_sem.at[mine], own_sem,
                     )
             return carry
 
@@ -409,24 +418,34 @@
         return carry
 
     lax.fori_loop(0, 4, part_of, 0)
-    pltpu.make_async_copy(spec_ref.at[0], spec_ref.at[0], spec_own).wait()
-    pltpu.make_async_remote_copy(
-        src_ref=spec_ref.at[pl.ds(0, 3)], dst_ref=spec_ref.at[pl.ds(0, 3)],
-        send_sem=spec_send, recv_sem=spec_recv, device_id=(lat, fld), device_id_type=MESH,
-    ).wait()
-    wait_all(recv_ref.at[0], recv_ref.at[pl.ds(0, 127)], send_sem, recv_sem, own_sem)
-
-
-def backward_kernel(inbox, angles_ref, slots_ref, modes_ref, out_ref, waves, line, modes, spread):
-    @pl.when(pl.program_id(0) == 0)
-    def _():
-        spread_waves(slots_ref, waves)
-        spread_modes(modes_ref, line, modes)
-
-        def gather(group, carry):
+    angle_load.wait()
+    here = jnp.where(lat < 16, lat // 4, (31 - lat) // 4)
+
+    def arrived(count, kind):
+        refs = inbox.at[pl.ds(0, count)]
+        pltpu.make_async_remote_copy(
+            src_ref=refs, dst_ref=refs, send_sem=send_sem, recv_sem=recv_sem.at[kind],
+            device_id=(lat, fld), device_id_type=MESH,
+        ).wait_recv()
+
+    for stage in range(4):
+        kind = lax.rem(here + 4 - stage, 4)
+
+        @pl.when(kind == mine)
+        def _():
+            pltpu.make_async_copy(inbox.at[0], inbox.at[0], own_sem).wait()
+            arrived(31, kind)
+
+        @pl.when(kind != mine)
+        def _():
+            arrived(32, kind)
+
+        first = (kind // 2) * 4 + 2 * lax.rem(kind, 2)
+
+        def gather(n, carry):
+            group = first + 8 * (n // 2) + lax.rem(n, 2)
             wave = waves[pl.ds(group, 1)]
-            cols = aligned(128 * group, 128, 128)
-
+            cols = aligned(128 * n, 128, 128)
             for q in range(5):
                 keep = wave < modes[16 * q : 16 * q + 16]
                 if q < 4:
@@ -442,23 +461,60 @@
                     ).astype(BF16)
             return carry
 
-        lax.fori_loop(0, GROUPS, gather, 0)
-
-    out_ref[...] = lax.dot_general(spread[...], angles_ref[...], NT, preferred_element_type=F32)
+        lax.fori_loop(0, 4, gather, 0)
+        if stage == 3:
+            rest_copy = pltpu.make_async_copy(spread, rest_ref, rest_sem)
+            rest_copy.start()
+            break
+
+        def add(n, carry):
+            rows = aligned(384 * n, 384, 128)
+            part = None
+            for half in range(2):
+                cols = aligned(128 * first + 1024 * half, 256, 256)
+                term = lax.dot_general(
+                    spread[:, 256 * half : 256 * half + 256], angles[rows, cols], NT,
+                    preferred_element_type=F32,
+                )
+                part = term if part is None else part + term
+            total[:, rows] = part if stage == 0 else total[:, rows] + part
+            if stage == 2:
+                pltpu.make_async_copy(total.at[:, rows], partial_ref.at[:, rows], out_sem).start()
+            return carry
+
+        lax.fori_loop(0, 7, add, 0)
+
+    pltpu.make_async_copy(total, partial_ref, out_sem).wait()
+    rest_copy.wait()
+    pltpu.make_async_copy(spec_ref.at[0], spec_ref.at[0], spec_own).wait()
+    pltpu.make_async_remote_copy(
+        src_ref=spec_ref.at[pl.ds(0, 3)], dst_ref=spec_ref.at[pl.ds(0, 3)],
+        send_sem=spec_send, recv_sem=spec_recv, device_id=(lat, fld), device_id_type=MESH,
+    ).wait()
+    others = inbox.at[pl.ds(0, 127)]
+    pltpu.make_async_remote_copy(
+        src_ref=others, dst_ref=others, send_sem=send_sem, recv_sem=recv_sem.at[0],
+        device_id=(lat, fld), device_id_type=MESH,
+    ).wait_send()
+
+
+def finish_kernel(first_ref, rest_ref, low_ref, high_ref, partial_ref, out_ref):
+    del first_ref
+    out_ref[...] = (
+        partial_ref[...]
+        + lax.dot_general(rest_ref[:, 0:256], low_ref[...], NT, preferred_element_type=F32)
+        + lax.dot_general(rest_ref[:, 256:512], high_ref[...], NT, preferred_element_type=F32)
+    )
 
 
 VMEM = pl.BlockSpec(memory_space=pltpu.VMEM)
 SMEM = pl.BlockSpec(memory_space=pltpu.SMEM)
 ANY = pl.BlockSpec(memory_space=pl.ANY)
-INBOX = jax.ShapeDtypeStruct((128, 64, 128), BF16)
 LIMIT = 60 * 1024 * 1024
 
 
-def whole(shape):
-    return pl.BlockSpec(shape, lambda i: (0,) * len(shape))
-
-
 def body(grid_in, legendre, wave_slot, lat_modes, gauss_weight, diffusion):
+    lat_index = lax.axis_index("lat")
     grid_rows = grid_in.reshape(640, LON)
     modes = lat_modes.reshape(1, 80)
     slots = wave_slot.reshape(6, 128)
@@ -491,12 +547,16 @@
         ),
     )(grid_rows, slots, modes)
 
-    returned, spectra = pl.pallas_call(
+    partial, rest, spectra = pl.pallas_call(
         middle_kernel,
         name="middle",
-        out_shape=(INBOX, jax.ShapeDtypeStruct((4, 6, 2, 8, 768), BF16)),
-        in_specs=[SMEM, ANY, ANY, VMEM, VMEM],
-        out_specs=(ANY, ANY),
+        out_shape=(
+            jax.ShapeDtypeStruct((640, LON), F32),
+            jax.ShapeDtypeStruct((640, 512), BF16),
+            jax.ShapeDtypeStruct((4, 6, 2, 8, 768), BF16),
+        ),
+        in_specs=[SMEM, ANY, ANY, VMEM, VMEM, VMEM, VMEM, ANY],
+        out_specs=(ANY, ANY, ANY),
         scratch_shapes=[
             pltpu.VMEM((2560, 512), BF16),
             pltpu.VMEM((6, 1280, 768), BF16),
@@ -510,34 +570,42 @@
             pltpu.VMEM((32, 128), F32),
             pltpu.VMEM((6, 64, 768), BF16),
             pltpu.VMEM((6, 2, 4, 8, 768), BF16),
+            pltpu.VMEM((GROUPS, 128), jnp.int32),
+            pltpu.VMEM((80, 128), jnp.int32),
+            pltpu.VMEM((LON, 2048), BF16),
+            pltpu.VMEM((640, LON), F32),
+            pltpu.VMEM((128, 64, 128), BF16),
+            pltpu.VMEM((640, 512), BF16),
         ]
-        + [pltpu.SemaphoreType.DMA] * 7
-        + [pltpu.SemaphoreType.DMA((6,))],
+        + [pltpu.SemaphoreType.DMA] * 9
+        + [pltpu.SemaphoreType.DMA((4,)), pltpu.SemaphoreType.DMA((6,))],
         compiler_params=pltpu.CompilerParams(
             collective_id=1, has_side_effects=True, vmem_limit_bytes=LIMIT
         ),
-    )(wave_slot, arrived, legendre, gauss_weight.reshape(10, 128), diffusion.reshape(1, 32))
-
+    )(
+        wave_slot, arrived, legendre, gauss_weight.reshape(10, 128), diffusion.reshape(1, 32),
+        slots, modes, angles,
+    )
+
+    last = lax.rem(jnp.where(lat_index < 16, lat_index // 4, (31 - lat_index) // 4) + 1, 4)
+    first = ((last // 2) * 2 + lax.rem(last, 2)).reshape(1)
     grid_out = pl.pallas_call(
-        backward_kernel,
-        name="backward",
-        grid=(7,),
+        finish_kernel,
+        name="finish",
+        grid_spec=pltpu.PrefetchScalarGridSpec(
+            num_scalar_prefetch=1,
+            grid=(7,),
+            in_specs=[
+                pl.BlockSpec((640, 512), lambda i, c: (0, 0)),
+                pl.BlockSpec((384, 256), lambda i, c: (i, c[0])),
+                pl.BlockSpec((384, 256), lambda i, c: (i, c[0] + 4)),
+                pl.BlockSpec((640, 384), lambda i, c: (0, i)),
+            ],
+            out_specs=pl.BlockSpec((640, 384), lambda i, c: (0, i)),
+        ),
         out_shape=jax.ShapeDtypeStruct((640, LON), F32),
-        in_specs=[
-            whole((128, 64, 128)),
-            pl.BlockSpec((384, 2048), lambda i: (i, 0)),
-            whole((6, 128)),
-            whole((1, 80)),
-        ],
-        out_specs=pl.BlockSpec((640, 384), lambda i: (0, i)),
-        scratch_shapes=[
-            pltpu.VMEM((GROUPS, 128), jnp.int32),
-            pltpu.VMEM((8, 128), F32),
-            pltpu.VMEM((80, 128), jnp.int32),
-            pltpu.VMEM((640, 2048), BF16),
-        ],
         compiler_params=pltpu.CompilerParams(vmem_limit_bytes=LIMIT),
-    )(returned, angles, slots, modes)
+    )(first, rest, angles, angles, partial)
 
     spectra = spectra.transpose(2, 0, 1, 3, 4).reshape(2, 24, 8, 768).astype(F32)
     return (grid_out.reshape(8, 80, LON), spectra)

time: 107 us -> 112 us (1.047)
  the two profiles are of different devices: /device:TPU:1 before, /device:TPU:7 now
where the time goes in v5:
time: 112 us
  Pallas kernels  110 us (98%)
    pallas_call x1, Pallas kernels, body(): pl.pallas_call(middle_kernel, name='middle', out_shape=(jax.ShapeDtypeStr...  58.6 us
    pallas_call x1, Pallas kernels, body(): pl.pallas_call(forward_kernel, name='forward', out_shape=(jax.ShapeDtypeS...  40 us
    pallas_call x1, Pallas kernels, body(): pl.pallas_call(finish_kernel, name='finish', grid_spec=pltpu.PrefetchScal...  11.1 us

profile of v5, /device:TPU:7, one launch (start us, length us, event | category | flops | bytes accessed | tf_op | source)
XLA Modules:
  0.0 111.7 jit_solution(15639644217148255747)
XLA Ops:
  0.7 40.0 %forward.1 = (bf16[2560,512]{1,0:T(8,128)(2,1)}, bf16[2688,2048]{1,0:T(8,128)(2,1)}) custom-call(bf16[640,2688]{1,0:T(8,128)(2,1)} %bitcast.12, s32[6,128]{1,0:T(8,128)} %bitcast.13, s32[1,80]{1,0:T(1,128)} %bitcast.16), custom_call_target="tpu_custom_call" | custom-call | tf_op jit(solution)/shard_map/forward/pallas_call | solution.py:522
  40.7 58.6 %middle.1 = (f32[640,2688]{1,0:T(8,128)}, bf16[640,512]{1,0:T(8,128)(2,1)}, bf16[4,6,2,8,768]{4,3,2,1,0:T(8,128)(2,1)}) custom-call(s32[768]{0:T(1024)} %slots_ref.1, bf16[2560,512]{1,0:T(8,128)(2,1)} %get-tuple-element.7.arrived_ref, bf16[6,1280,768]{2,1,0:T(8,128)(2,1)} %tables_ref.1, f32[10,128]{1,0:T(8,128)} %bitcast.15, f32[1,32]{1,0:T(1,128)} %bitcast.18, ...), custom_call_target="tpu_custom_call" | custom-call | tf_op jit(solution)/shard_map/middle/pallas_call | solution.py:550
  99.3 0.0 copy-start
  99.4 11.1 %finish.1 = f32[640,2688]{1,0:T(8,128)} custom-call(s32[1]{0:T(128)} %bitcast.first_ref, bf16[640,512]{1,0:T(8,128)(2,1)} %get-tuple-element.9.rest_ref, bf16[2688,2048]{1,0:T(8,128)(2,1)} %get-tuple-element.8.angles_ref.low_ref.high_ref, bf16[2688,2048]{1,0:T(8,128)(2,1)} %get-tuple-element.8.angles_ref.low_ref.high_ref, ...), custom_call_target="tpu_custom_call" | custom-call | tf_op jit(solution)/shard_map/finish/pallas_call | solution.py:592
  110.5 0.0 copy-done
  110.5 0.1 convert_element_type.13
  110.6 1.1 copy.8
Async XLA Ops:
  99.3 11.2 %copy-start = (bf16[4,6,2,8,768]{4,3,2,1,0:T(8,128)(2,1)S(1)}, bf16[4,6,2,8,768]{4,3,2,1,0:T(8,128)(2,1)}, u32[]{:S(2)}) copy-start(bf16[4,6,2,8,768]{4,3,2,1,0:T(8,128)(2,1)} %get-tuple-element.11) | copy-start | bytes 1769476

commit v6 on v5

--- a/solution.py
+++ b/solution.py
@@ -273,11 +273,11 @@
 
 
 def middle_kernel(
-    slots_ref, arrived_ref, tables_ref, weight_ref, rate_ref, rows_ref, modes_ref, angles_ref,
-    partial_ref, rest_ref, spec_ref,
+    slots_ref, arrived_ref, tables_ref, weight_ref, rate_ref, rows_ref, modes_ref,
+    spread_ref, spec_ref,
     wide, tables, even, odd, north, south, pick, place, line, rates, coeff, spec_box,
-    waves, modes, angles, total, inbox, spread,
-    send_sem, own_sem, spec_send, spec_recv, spec_own, wide_sem, angle_sem, out_sem, rest_sem,
+    waves, modes, inbox, spread,
+    send_sem, own_sem, spec_send, spec_recv, spec_own, wide_sem, out_sem,
     recv_sem, table_sem,
 ):
     z, x, lat, fld = position()
@@ -312,24 +312,27 @@
 
     lax.fori_loop(0, 8, unpack, 0)
     flip = flip_matrix(256)
+    downs = [
+        jnp.dot(flip, wide[2304 - 256 * b : 2560 - 256 * b], preferred_element_type=F32)
+        for b in range(5)
+    ]
     for b in range(5):
         up = wide[256 * b : 256 * b + 256].astype(F32)
-        low = 1280 + 256 * (4 - b)
-        down = jnp.dot(flip, wide[low : low + 256], preferred_element_type=F32)
         weight = jnp.concatenate(
             [as_column(weight_ref[2 * b + u : 2 * b + u + 1])[:, 0:1] for u in range(2)], 0
         )
-        for target, value in ((even, up + down), (odd, up - down)):
+        for target, value in ((even, up + downs[b]), (odd, up - downs[b])):
             target[:, 256 * b : 256 * b + 256] = lax.dot_general(
                 pick[...], (value * weight).astype(BF16), NT, preferred_element_type=F32
             ).astype(BF16)
 
-    col = lax.broadcasted_iota(jnp.int32, (32, 384), 1)
     for slot in range(6):
+        used = 256 if slot % 2 else 384
+        col = lax.broadcasted_iota(jnp.int32, (32, used), 1)
         table_loads[slot].wait()
         wave = slots_ref[me * 6 + slot]
         for parity, source in enumerate((even, odd)):
-            cols = slice(384 * parity, 384 * parity + 384)
+            cols = slice(384 * parity, 384 * parity + used)
             raw = jnp.dot(
                 source[64 * slot : 64 * slot + 64], tables[slot, :, cols],
                 preferred_element_type=F32,
@@ -345,11 +348,12 @@
                     low = 32 * r + 8 * k
                     spec_box[slot, r, k, :, cols] = value[low : low + 8].astype(BF16)
             coeff[slot, :, cols] = value.astype(BF16)
+            if used < 384:
+                spec_box[slot, :, :, :, 384 * parity + used : 384 * parity + 384] = jnp.zeros(
+                    (2, 4, 8, 384 - used), BF16
+                )
         if slot == 0:
             greeted()
-        if slot == 5:
-            angle_load = pltpu.make_async_copy(angles_ref, angles, angle_sem)
-            angle_load.start()
         for shift in range(4):
             to = lax.rem(fld + shift, 4)
             source, target = spec_box.at[slot, :, to], spec_ref.at[fld, slot]
@@ -368,10 +372,11 @@
     def part_of(step, carry):
         b = lax.rem(step + mine, 4)
         for slot in range(6):
+            used = 256 if slot % 2 else 384
             sums = [
                 lax.dot_general(
-                    tables[slot, aligned(320 * b, 320, 64), 384 * p : 384 * p + 384],
-                    coeff[slot, :, 384 * p : 384 * p + 384],
+                    tables[slot, aligned(320 * b, 320, 64), 384 * p : 384 * p + used],
+                    coeff[slot, :, 384 * p : 384 * p + used],
                     NT,
                     preferred_element_type=F32,
                 )
@@ -418,7 +423,6 @@
         return carry
 
     lax.fori_loop(0, 4, part_of, 0)
-    angle_load.wait()
     here = jnp.where(lat < 16, lat // 4, (31 - lat) // 4)
 
     def arrived(count, kind):
@@ -445,7 +449,7 @@
         def gather(n, carry):
             group = first + 8 * (n // 2) + lax.rem(n, 2)
             wave = waves[pl.ds(group, 1)]
-            cols = aligned(128 * n, 128, 128)
+            cols = aligned(128 * group, 128, 128)
             for q in range(5):
                 keep = wave < modes[16 * q : 16 * q + 16]
                 if q < 4:
@@ -462,30 +466,11 @@
             return carry
 
         lax.fori_loop(0, 4, gather, 0)
-        if stage == 3:
-            rest_copy = pltpu.make_async_copy(spread, rest_ref, rest_sem)
-            rest_copy.start()
-            break
-
-        def add(n, carry):
-            rows = aligned(384 * n, 384, 128)
-            part = None
-            for half in range(2):
-                cols = aligned(128 * first + 1024 * half, 256, 256)
-                term = lax.dot_general(
-                    spread[:, 256 * half : 256 * half + 256], angles[rows, cols], NT,
-                    preferred_element_type=F32,
-                )
-                part = term if part is None else part + term
-            total[:, rows] = part if stage == 0 else total[:, rows] + part
-            if stage == 2:
-                pltpu.make_async_copy(total.at[:, rows], partial_ref.at[:, rows], out_sem).start()
-            return carry
-
-        lax.fori_loop(0, 7, add, 0)
-
-    pltpu.make_async_copy(total, partial_ref, out_sem).wait()
-    rest_copy.wait()
+        for half in range(2):
+            cols = aligned(128 * first + 1024 * half, 256, 256)
+            pltpu.make_async_copy(spread.at[:, cols], spread_ref.at[:, cols], out_sem).start()
+
+    pltpu.make_async_copy(spread, spread_ref, out_sem).wait()
     pltpu.make_async_copy(spec_ref.at[0], spec_ref.at[0], spec_own).wait()
     pltpu.make_async_remote_copy(
         src_ref=spec_ref.at[pl.ds(0, 3)], dst_ref=spec_ref.at[pl.ds(0, 3)],
@@ -498,15 +483,6 @@
     ).wait_send()
 
 
-def finish_kernel(first_ref, rest_ref, low_ref, high_ref, partial_ref, out_ref):
-    del first_ref
-    out_ref[...] = (
-        partial_ref[...]
-        + lax.dot_general(rest_ref[:, 0:256], low_ref[...], NT, preferred_element_type=F32)
-        + lax.dot_general(rest_ref[:, 256:512], high_ref[...], NT, preferred_element_type=F32)
-    )
-
-
 VMEM = pl.BlockSpec(memory_space=pltpu.VMEM)
 SMEM = pl.BlockSpec(memory_space=pltpu.SMEM)
 ANY = pl.BlockSpec(memory_space=pl.ANY)
@@ -514,7 +490,6 @@
 
 
 def body(grid_in, legendre, wave_slot, lat_modes, gauss_weight, diffusion):
-    lat_index = lax.axis_index("lat")
     grid_rows = grid_in.reshape(640, LON)
     modes = lat_modes.reshape(1, 80)
     slots = wave_slot.reshape(6, 128)
@@ -547,16 +522,15 @@
         ),
     )(grid_rows, slots, modes)
 
-    partial, rest, spectra = pl.pallas_call(
+    spread, spectra = pl.pallas_call(
         middle_kernel,
         name="middle",
         out_shape=(
-            jax.ShapeDtypeStruct((640, LON), F32),
-            jax.ShapeDtypeStruct((640, 512), BF16),
+            jax.ShapeDtypeStruct((640, 2048), BF16),
             jax.ShapeDtypeStruct((4, 6, 2, 8, 768), BF16),
         ),
-        in_specs=[SMEM, ANY, ANY, VMEM, VMEM, VMEM, VMEM, ANY],
-        out_specs=(ANY, ANY, ANY),
+        in_specs=[SMEM, ANY, ANY, VMEM, VMEM, VMEM, VMEM],
+        out_specs=(ANY, ANY),
         scratch_shapes=[
             pltpu.VMEM((2560, 512), BF16),
             pltpu.VMEM((6, 1280, 768), BF16),
@@ -572,40 +546,20 @@
             pltpu.VMEM((6, 2, 4, 8, 768), BF16),
             pltpu.VMEM((GROUPS, 128), jnp.int32),
             pltpu.VMEM((80, 128), jnp.int32),
-            pltpu.VMEM((LON, 2048), BF16),
-            pltpu.VMEM((640, LON), F32),
             pltpu.VMEM((128, 64, 128), BF16),
-            pltpu.VMEM((640, 512), BF16),
+            pltpu.VMEM((640, 2048), BF16),
         ]
-        + [pltpu.SemaphoreType.DMA] * 9
+        + [pltpu.SemaphoreType.DMA] * 7
         + [pltpu.SemaphoreType.DMA((4,)), pltpu.SemaphoreType.DMA((6,))],
         compiler_params=pltpu.CompilerParams(
             collective_id=1, has_side_effects=True, vmem_limit_bytes=LIMIT
         ),
     )(
         wave_slot, arrived, legendre, gauss_weight.reshape(10, 128), diffusion.reshape(1, 32),
-        slots, modes, angles,
+        slots, modes,
     )
 
-    last = lax.rem(jnp.where(lat_index < 16, lat_index // 4, (31 - lat_index) // 4) + 1, 4)
-    first = ((last // 2) * 2 + lax.rem(last, 2)).reshape(1)
-    grid_out = pl.pallas_call(
-        finish_kernel,
-        name="finish",
-        grid_spec=pltpu.PrefetchScalarGridSpec(
-            num_scalar_prefetch=1,
-            grid=(7,),
-            in_specs=[
-                pl.BlockSpec((640, 512), lambda i, c: (0, 0)),
-                pl.BlockSpec((384, 256), lambda i, c: (i, c[0])),
-                pl.BlockSpec((384, 256), lambda i, c: (i, c[0] + 4)),
-                pl.BlockSpec((640, 384), lambda i, c: (0, i)),
-            ],
-            out_specs=pl.BlockSpec((640, 384), lambda i, c: (0, i)),
-        ),
-        out_shape=jax.ShapeDtypeStruct((640, LON), F32),
-        compiler_params=pltpu.CompilerParams(vmem_limit_bytes=LIMIT),
-    )(first, rest, angles, angles, partial)
+    grid_out = lax.dot_general(spread, angles, NT, preferred_element_type=F32)
 
     spectra = spectra.transpose(2, 0, 1, 3, 4).reshape(2, 24, 8, 768).astype(F32)
     return (grid_out.reshape(8, 80, LON), spectra)

time: 112 us -> 104 us (0.929)
  the two profiles are of different devices: /device:TPU:7 before, /device:TPU:1 now
where the time goes in v6:
time: 104 us; the launch traced here: 103 us
  Pallas kernels  86.5 us (83%)
  matrix products  14.2 us (14%)
  local copies, waits for them, and re-layouts  1.1 us (1%)
    pallas_call x1, Pallas kernels, body(): pl.pallas_call(middle_kernel, name='middle', out_shape=(jax.ShapeDtypeStr...  44.1 us
    pallas_call x1, Pallas kernels, body(): pl.pallas_call(forward_kernel, name='forward', out_shape=(jax.ShapeDtypeS...  42.4 us
    dot_general x1, matrix products, body(): grid_out = lax.dot_general(spread, angles, NT, preferred_element_type=F32)  14.2 us

profile of v6, /device:TPU:1, one launch (start us, length us, event | category | flops | bytes accessed | tf_op | source)
XLA Modules:
  0.0 102.6 jit_solution(7059452973390419484)
XLA Ops:
  0.6 42.4 %forward.1 = (bf16[2560,512]{1,0:T(8,128)(2,1)}, bf16[2688,2048]{1,0:T(8,128)(2,1)}) custom-call(bf16[640,2688]{1,0:T(8,128)(2,1)} %bitcast.12, s32[6,128]{1,0:T(8,128)} %bitcast.13, s32[1,80]{1,0:T(1,128)} %bitcast.16), custom_call_target="tpu_custom_call" | custom-call | tf_op jit(solution)/shard_map/forward/pallas_call | solution.py:497
  43.1 44.1 %middle.1 = (bf16[640,2048]{1,0:T(8,128)(2,1)}, bf16[4,6,2,8,768]{4,3,2,1,0:T(8,128)(2,1)}) custom-call(s32[768]{0:T(1024)} %slots_ref.1, bf16[2560,512]{1,0:T(8,128)(2,1)} %get-tuple-element.6.arrived_ref, bf16[6,1280,768]{2,1,0:T(8,128)(2,1)} %tables_ref.1, f32[10,128]{1,0:T(8,128)} %bitcast.15, f32[1,32]{1,0:T(1,128)} %bitcast.18, s32[6,128]{1,0:T(8,128)} %bitcast.14, ...), custom_call_target="tpu_custom_call" | custom-call | tf_op jit(solution)/shard_map/middle/pallas_call | solution.py:525
  87.2 0.0 copy-start
  87.2 14.2 %fusion = f32[640,2688]{1,0:T(8,128)} fusion(bf16[640,2048]{1,0:T(8,128)(2,1)} %get-tuple-element.7, bf16[2688,2048]{1,0:T(8,128)(2,1)} %get-tuple-element.8), kind=kOutput, calls=%fused_computation | convolution fusion | flops 7046430720 | bytes 20512768 | tf_op jit(solution)/shard_map/dot_general | solution.py:562
  101.4 0.0 copy-done
  101.4 0.1 convert_element_type.13
  101.5 1.1 %copy.8 = f32[2,24,8,768]{3,2,1,0:T(8,128)} copy(f32[2,24,8,768]{3,2,0,1:T(8,128)S(1)} %bitcast.11) | data formatting | bytes 2359296
Async XLA Ops:
  87.2 14.2 %copy-start = (bf16[4,6,2,8,768]{4,3,2,1,0:T(8,128)(2,1)S(1)}, bf16[4,6,2,8,768]{4,3,2,1,0:T(8,128)(2,1)}, u32[]{:S(2)}) copy-start(bf16[4,6,2,8,768]{4,3,2,1,0:T(8,128)(2,1)} %get-tuple-element.9) | copy-start | bytes 1769476

commit v7 on v6

--- a/solution.py
+++ b/solution.py
@@ -164,12 +164,11 @@
     lax.fori_loop(0, ROW_A, rows, 0)
 
 
-def forward_kernel(
-    grid_ref, slots_ref, modes_ref, recv_ref, angles_ref,
+def forward_part(
+    grid_ref, slots_ref, modes_ref, landing_ref, angles_ref,
     waves, line, modes, trig, uv, table, result, outbox,
     send_sem, recv_sem, own_sem, table_sem,
 ):
-    greet()
     lane16 = lax.rem(lanes(), 16)
     spread_waves(slots_ref, waves)
     spread_modes(modes_ref, line, modes)
@@ -218,7 +217,7 @@
             greeted()
 
         _, _, lat, fld = position()
-        landing = recv_ref.at[aligned(80 * lat, 64), aligned(128 * fld, 128, 128)]
+        landing = landing_ref.at[aligned(80 * lat, 64), aligned(128 * fld, 128, 128)]
         for half in range(2):
             def send(n, carry):
                 to = groups[half] * 8 + n
@@ -229,9 +228,6 @@
         return carry
 
     lax.fori_loop(0, GROUPS // 2, step_body, 0)
-    wait_all(
-        outbox.at[0], recv_ref.at[pl.ds(0, 2032)], send_sem, recv_sem, own_sem
-    )
 
 
 def unpack_last(read):
@@ -272,31 +268,35 @@
     lax.fori_loop(0, 8, lanes_of, 0)
 
 
-def middle_kernel(
-    slots_ref, arrived_ref, tables_ref, weight_ref, rate_ref, rows_ref, modes_ref,
-    spread_ref, spec_ref,
+def exchange_kernel(
+    wave_ref, grid_ref, tables_ref, weight_ref, rate_ref, rows_ref, modes_ref,
+    angles_ref, spread_ref, spec_ref,
+    trig, uv, table, result, outbox,
     wide, tables, even, odd, north, south, pick, place, line, rates, coeff, spec_box,
     waves, modes, inbox, spread,
-    send_sem, own_sem, spec_send, spec_recv, spec_own, wide_sem, out_sem,
-    recv_sem, table_sem,
+    first_send, first_recv, first_own, send_sem, own_sem, spec_send, spec_recv, spec_own, out_sem,
+    angle_sem, recv_sem, table_sem,
 ):
     z, x, lat, fld = position()
     me = lat * 4 + fld
-    load = pltpu.make_async_copy(arrived_ref, wide, wide_sem)
-    load.start()
+    greet()
     table_loads = [
         pltpu.make_async_copy(tables_ref.at[s], tables.at[s], table_sem.at[s]) for s in range(6)
     ]
     for copy in table_loads:
         copy.start()
-    greet()
+    forward_part(
+        grid_ref, rows_ref, modes_ref, wide, angles_ref,
+        waves, line, modes, trig, uv, table, result, outbox,
+        first_send, first_recv, first_own, angle_sem,
+    )
     fill_picks(pick, place)
     line[...] = jnp.zeros((8, 128), F32)
     line[0:1, 0:32] = rate_ref[...]
     rates[...] = as_column(line[0:1])[0:32]
-    spread_waves(rows_ref, waves)
-    spread_modes(modes_ref, line, modes)
-    load.wait()
+    for copy in table_loads:
+        copy.wait()
+    wait_all(outbox.at[0], wide.at[pl.ds(0, 2032)], first_send, first_recv, first_own)
 
     def unpack(n, carry):
         done = []
@@ -329,8 +329,7 @@
     for slot in range(6):
         used = 256 if slot % 2 else 384
         col = lax.broadcasted_iota(jnp.int32, (32, used), 1)
-        table_loads[slot].wait()
-        wave = slots_ref[me * 6 + slot]
+        wave = wave_ref[me * 6 + slot]
         for parity, source in enumerate((even, odd)):
             cols = slice(384 * parity, 384 * parity + used)
             raw = jnp.dot(
@@ -352,8 +351,6 @@
                 spec_box[slot, :, :, :, 384 * parity + used : 384 * parity + 384] = jnp.zeros(
                     (2, 4, 8, 384 - used), BF16
                 )
-        if slot == 0:
-            greeted()
         for shift in range(4):
             to = lax.rem(fld + shift, 4)
             source, target = spec_box.at[slot, :, to], spec_ref.at[fld, slot]
@@ -483,6 +480,17 @@
     ).wait_send()
 
 
+def backward_kernel(spread_ref, angles_ref, spec_ref, out_ref, spectra_ref):
+    out_ref[...] = lax.dot_general(spread_ref[...], angles_ref[...], NT, preferred_element_type=F32)
+
+    @pl.when(pl.program_id(0) == 0)
+    def _():
+        for k in range(4):
+            for slot in range(6):
+                for r in range(2):
+                    spectra_ref[r, 6 * k + slot] = spec_ref[k, slot, r].astype(F32)
+
+
 VMEM = pl.BlockSpec(memory_space=pltpu.VMEM)
 SMEM = pl.BlockSpec(memory_space=pltpu.SMEM)
 ANY = pl.BlockSpec(memory_space=pl.ANY)
@@ -494,44 +502,22 @@
     modes = lat_modes.reshape(1, 80)
     slots = wave_slot.reshape(6, 128)
 
-    arrived, angles = pl.pallas_call(
-        forward_kernel,
-        name="forward",
+    angles, spread, spectra = pl.pallas_call(
+        exchange_kernel,
+        name="exchange",
         out_shape=(
-            jax.ShapeDtypeStruct((2560, 512), BF16),
             jax.ShapeDtypeStruct((LON, 2048), BF16),
+            jax.ShapeDtypeStruct((640, 2048), BF16),
+            jax.ShapeDtypeStruct((4, 6, 2, 8, 768), BF16),
         ),
-        in_specs=[VMEM] * 3,
-        out_specs=(ANY, ANY),
+        in_specs=[SMEM, VMEM, ANY, VMEM, VMEM, VMEM, VMEM],
+        out_specs=(ANY, ANY, ANY),
         scratch_shapes=[
-            pltpu.VMEM((GROUPS, 128), jnp.int32),
-            pltpu.VMEM((8, 128), F32),
-            pltpu.VMEM((80, 128), jnp.int32),
             pltpu.VMEM((2, GROUPS, TRIG_ROWS, 128), F32),
             pltpu.VMEM((2, 192, 128), F32),
             pltpu.VMEM((LON, 256), BF16),
             pltpu.VMEM((640, 256), F32),
             pltpu.VMEM((128, 64, 128), BF16),
-            pltpu.SemaphoreType.DMA,
-            pltpu.SemaphoreType.DMA,
-            pltpu.SemaphoreType.DMA,
-            pltpu.SemaphoreType.DMA((2,)),
-        ],
-        compiler_params=pltpu.CompilerParams(
-            collective_id=0, has_side_effects=True, vmem_limit_bytes=LIMIT
-        ),
-    )(grid_rows, slots, modes)
-
-    spread, spectra = pl.pallas_call(
-        middle_kernel,
-        name="middle",
-        out_shape=(
-            jax.ShapeDtypeStruct((640, 2048), BF16),
-            jax.ShapeDtypeStruct((4, 6, 2, 8, 768), BF16),
-        ),
-        in_specs=[SMEM, ANY, ANY, VMEM, VMEM, VMEM, VMEM],
-        out_specs=(ANY, ANY),
-        scratch_shapes=[
             pltpu.VMEM((2560, 512), BF16),
             pltpu.VMEM((6, 1280, 768), BF16),
             pltpu.VMEM((384, 1280), BF16),
@@ -549,19 +535,40 @@
             pltpu.VMEM((128, 64, 128), BF16),
             pltpu.VMEM((640, 2048), BF16),
         ]
-        + [pltpu.SemaphoreType.DMA] * 7
-        + [pltpu.SemaphoreType.DMA((4,)), pltpu.SemaphoreType.DMA((6,))],
+        + [pltpu.SemaphoreType.DMA] * 9
+        + [
+            pltpu.SemaphoreType.DMA((2,)),
+            pltpu.SemaphoreType.DMA((4,)),
+            pltpu.SemaphoreType.DMA((6,)),
+        ],
         compiler_params=pltpu.CompilerParams(
-            collective_id=1, has_side_effects=True, vmem_limit_bytes=LIMIT
+            collective_id=0, has_side_effects=True, vmem_limit_bytes=LIMIT
         ),
     )(
-        wave_slot, arrived, legendre, gauss_weight.reshape(10, 128), diffusion.reshape(1, 32),
+        wave_slot, grid_rows, legendre, gauss_weight.reshape(10, 128), diffusion.reshape(1, 32),
         slots, modes,
     )
 
-    grid_out = lax.dot_general(spread, angles, NT, preferred_element_type=F32)
-
-    spectra = spectra.transpose(2, 0, 1, 3, 4).reshape(2, 24, 8, 768).astype(F32)
+    grid_out, spectra = pl.pallas_call(
+        backward_kernel,
+        name="backward",
+        grid=(3,),
+        out_shape=(
+            jax.ShapeDtypeStruct((640, LON), F32),
+            jax.ShapeDtypeStruct((2, 24, 8, 768), F32),
+        ),
+        in_specs=[
+            pl.BlockSpec((640, 2048), lambda i: (0, 0)),
+            pl.BlockSpec((896, 2048), lambda i: (i, 0)),
+            pl.BlockSpec((4, 6, 2, 8, 768), lambda i: (0, 0, 0, 0, 0)),
+        ],
+        out_specs=(
+            pl.BlockSpec((640, 896), lambda i: (0, i)),
+            pl.BlockSpec((2, 24, 8, 768), lambda i: (0, 0, 0, 0)),
+        ),
+        compiler_params=pltpu.CompilerParams(vmem_limit_bytes=LIMIT),
+    )(spread, angles, spectra)
+
     return (grid_out.reshape(8, 80, LON), spectra)
 
 

time: 104 us -> 98 us (0.942)
  matrix products: 14.2 us -> 0 us
  Pallas kernels: 86.5 us -> 96.6 us
  local copies, waits for them, and re-layouts: 1.1 us -> 0 us
    dot_general x1 -> x0, matrix products: 14.2 us -> none  [body(): grid_out = lax.dot_general(spread, angles, NT, preferred_element_type=F32)]
    pallas_call x2, Pallas kernels: 86.5 us -> 96.6 us  [the longest x1 83.1 us: body(): pl.pallas_call(exchange_kernel, name='exchange', out_shape=(jax.ShapeDtyp...]
    unnamed x3 -> x0, local copies, waits for them, and re-layouts: 1.1 us -> none
where the time goes in v7:
time: 98 us; the launch traced here: 97.2 us
  Pallas kernels  96.6 us (99%)
    pallas_call x1, Pallas kernels, body(): pl.pallas_call(exchange_kernel, name='exchange', out_shape=(jax.ShapeDtyp...  83.1 us
    pallas_call x1, Pallas kernels, body(): pl.pallas_call(backward_kernel, name='backward', grid=(3,), out_shape=(ja...  13.5 us

profile of v7, /device:TPU:1, one launch (start us, length us, event | category | flops | bytes accessed | tf_op | source)
XLA Modules:
  0.0 97.2 jit_solution(10056318057011187132)
XLA Ops:
  0.6 83.1 %exchange.1 = (bf16[2688,2048]{1,0:T(8,128)(2,1)}, bf16[640,2048]{1,0:T(8,128)(2,1)}, bf16[4,6,2,8,768]{4,3,2,1,0:T(8,128)(2,1)}) custom-call(s32[768]{0:T(1024)} %wave_ref.1, bf16[640,2688]{1,0:T(8,128)(2,1)} %bitcast.6, bf16[6,1280,768]{2,1,0:T(8,128)(2,1)} %tables_ref.1, f32[10,128]{1,0:T(8,128)} %bitcast.8, f32[1,32]{1,0:T(1,128)} %bitcast.9, ...), custom_call_target="tpu_custom_call" | custom-call | tf_op jit(solution)/shard_map/exchange/pallas_call | solution.py:505
  83.7 13.5 %backward.1 = (f32[640,2688]{1,0:T(8,128)}, f32[2,24,8,768]{3,2,1,0:T(8,128)}) custom-call(bf16[640,2048]{1,0:T(8,128)(2,1)} %get-tuple-element.7.spread_ref, bf16[2688,2048]{1,0:T(8,128)(2,1)} %get-tuple-element.8.angles_ref, bf16[4,6,2,8,768]{4,3,2,1,0:T(8,128)(2,1)} %get-tuple-element.9.spec_ref), custom_call_target="tpu_custom_call" | custom-call | tf_op jit(solution)/shard_map/backward/pallas_call | solution.py:552

commit v8 on v7

--- a/solution.py
+++ b/solution.py
@@ -270,11 +270,11 @@
 
 def exchange_kernel(
     wave_ref, grid_ref, tables_ref, weight_ref, rate_ref, rows_ref, modes_ref,
-    angles_ref, spread_ref, spec_ref,
+    angles_ref, partial_ref, rest_ref, spec_ref,
     trig, uv, table, result, outbox,
     wide, tables, even, odd, north, south, pick, place, line, rates, coeff, spec_box,
-    waves, modes, inbox, spread,
-    first_send, first_recv, first_own, send_sem, own_sem, spec_send, spec_recv, spec_own, out_sem,
+    waves, modes, inbox, spread, early, total,
+    first_send, first_recv, first_own, send_sem, own_sem, spec_send, spec_recv, spec_own, out_sem, rest_sem, early_sem,
     angle_sem, recv_sem, table_sem,
 ):
     z, x, lat, fld = position()
@@ -297,6 +297,18 @@
     for copy in table_loads:
         copy.wait()
     wait_all(outbox.at[0], wide.at[pl.ds(0, 2032)], first_send, first_recv, first_own)
+    mine = 2 * lax.rem(z, 2) + x // 2
+    here = jnp.where(lat < 16, lat // 4, (31 - lat) // 4)
+    kinds = [lax.rem(here + 4 - stage, 4) for stage in range(4)]
+    firsts = [(kind // 2) * 4 + 2 * lax.rem(kind, 2) for kind in kinds]
+    for stage in range(2):
+        for half in range(2):
+            low = 512 * stage + 256 * half
+            pltpu.make_async_copy(
+                angles_ref.at[:, aligned(128 * firsts[stage] + 1024 * half, 256, 256)],
+                early.at[:, low : low + 256],
+                early_sem,
+            ).start()
 
     def unpack(n, carry):
         done = []
@@ -362,7 +374,6 @@
             else:
                 pltpu.make_async_copy(source, target, spec_own).start()
 
-    mine = 2 * lax.rem(z, 2) + x // 2
     turn = flip_matrix(320)
     lane16 = lax.rem(lanes(), 16)
 
@@ -420,7 +431,6 @@
         return carry
 
     lax.fori_loop(0, 4, part_of, 0)
-    here = jnp.where(lat < 16, lat // 4, (31 - lat) // 4)
 
     def arrived(count, kind):
         refs = inbox.at[pl.ds(0, count)]
@@ -430,7 +440,7 @@
         ).wait_recv()
 
     for stage in range(4):
-        kind = lax.rem(here + 4 - stage, 4)
+        kind, first = kinds[stage], firsts[stage]
 
         @pl.when(kind == mine)
         def _():
@@ -441,12 +451,10 @@
         def _():
             arrived(32, kind)
 
-        first = (kind // 2) * 4 + 2 * lax.rem(kind, 2)
-
         def gather(n, carry):
             group = first + 8 * (n // 2) + lax.rem(n, 2)
             wave = waves[pl.ds(group, 1)]
-            cols = aligned(128 * group, 128, 128)
+            cols = aligned(512 * stage + 128 * n, 128, 128)
             for q in range(5):
                 keep = wave < modes[16 * q : 16 * q + 16]
                 if q < 4:
@@ -463,11 +471,26 @@
             return carry
 
         lax.fori_loop(0, 4, gather, 0)
-        for half in range(2):
-            cols = aligned(128 * first + 1024 * half, 256, 256)
-            pltpu.make_async_copy(spread.at[:, cols], spread_ref.at[:, cols], out_sem).start()
-
-    pltpu.make_async_copy(spread, spread_ref, out_sem).wait()
+        if stage == 1:
+            pltpu.make_async_copy(early, early, early_sem).wait()
+
+            def begin(n, carry):
+                rows = aligned(896 * n, 896, 128)
+                total[:, rows] = lax.dot_general(
+                    spread[:, 0:1024], early[rows], NT, preferred_element_type=F32
+                )
+                pltpu.make_async_copy(total.at[:, rows], partial_ref.at[:, rows], out_sem).start()
+                return carry
+
+            lax.fori_loop(0, 3, begin, 0)
+        if stage >= 2:
+            low = 512 * stage
+            pltpu.make_async_copy(
+                spread.at[:, low : low + 512], rest_ref.at[:, low - 1024 : low - 512], rest_sem
+            ).start()
+
+    pltpu.make_async_copy(total, partial_ref, out_sem).wait()
+    pltpu.make_async_copy(rest_ref, rest_ref, rest_sem).wait()
     pltpu.make_async_copy(spec_ref.at[0], spec_ref.at[0], spec_own).wait()
     pltpu.make_async_remote_copy(
         src_ref=spec_ref.at[pl.ds(0, 3)], dst_ref=spec_ref.at[pl.ds(0, 3)],
@@ -480,8 +503,16 @@
     ).wait_send()
 
 
-def backward_kernel(spread_ref, angles_ref, spec_ref, out_ref, spectra_ref):
-    out_ref[...] = lax.dot_general(spread_ref[...], angles_ref[...], NT, preferred_element_type=F32)
+def backward_kernel(
+    firsts_ref, rest_ref, a_ref, b_ref, c_ref, d_ref, partial_ref, spec_ref,
+    out_ref, spectra_ref, late,
+):
+    del firsts_ref
+    for n, ref in enumerate((a_ref, b_ref, c_ref, d_ref)):
+        late[:, 256 * n : 256 * n + 256] = ref[...]
+    out_ref[...] = partial_ref[...] + lax.dot_general(
+        rest_ref[...], late[...], NT, preferred_element_type=F32
+    )
 
     @pl.when(pl.program_id(0) == 0)
     def _():
@@ -502,16 +533,17 @@
     modes = lat_modes.reshape(1, 80)
     slots = wave_slot.reshape(6, 128)
 
-    angles, spread, spectra = pl.pallas_call(
+    angles, partial, rest, spectra = pl.pallas_call(
         exchange_kernel,
         name="exchange",
         out_shape=(
             jax.ShapeDtypeStruct((LON, 2048), BF16),
-            jax.ShapeDtypeStruct((640, 2048), BF16),
+            jax.ShapeDtypeStruct((640, LON), F32),
+            jax.ShapeDtypeStruct((640, 1024), BF16),
             jax.ShapeDtypeStruct((4, 6, 2, 8, 768), BF16),
         ),
         in_specs=[SMEM, VMEM, ANY, VMEM, VMEM, VMEM, VMEM],
-        out_specs=(ANY, ANY, ANY),
+        out_specs=(ANY, ANY, ANY, ANY),
         scratch_shapes=[
             pltpu.VMEM((2, GROUPS, TRIG_ROWS, 128), F32),
             pltpu.VMEM((2, 192, 128), F32),
@@ -534,8 +566,10 @@
             pltpu.VMEM((80, 128), jnp.int32),
             pltpu.VMEM((128, 64, 128), BF16),
             pltpu.VMEM((640, 2048), BF16),
+            pltpu.VMEM((LON, 1024), BF16),
+            pltpu.VMEM((640, LON), F32),
         ]
-        + [pltpu.SemaphoreType.DMA] * 9
+        + [pltpu.SemaphoreType.DMA] * 11
         + [
             pltpu.SemaphoreType.DMA((2,)),
             pltpu.SemaphoreType.DMA((4,)),
@@ -549,25 +583,41 @@
         slots, modes,
     )
 
+    lat = lax.axis_index("lat")
+    here = jnp.where(lat < 16, lat // 4, (31 - lat) // 4)
+    late = (here + jnp.array([2, 1], jnp.int32)) % 4
+    firsts = (late // 2) * 2 + late % 2
+
+    def table_block(stage, half):
+        return pl.BlockSpec((896, 256), lambda i, c: (i, c[stage] + 4 * half))
+
     grid_out, spectra = pl.pallas_call(
         backward_kernel,
         name="backward",
-        grid=(3,),
+        grid_spec=pltpu.PrefetchScalarGridSpec(
+            num_scalar_prefetch=1,
+            grid=(3,),
+            in_specs=[
+                pl.BlockSpec((640, 1024), lambda i, c: (0, 0)),
+                table_block(0, 0),
+                table_block(0, 1),
+                table_block(1, 0),
+                table_block(1, 1),
+                pl.BlockSpec((640, 896), lambda i, c: (0, i)),
+                pl.BlockSpec((4, 6, 2, 8, 768), lambda i, c: (0, 0, 0, 0, 0)),
+            ],
+            out_specs=(
+                pl.BlockSpec((640, 896), lambda i, c: (0, i)),
+                pl.BlockSpec((2, 24, 8, 768), lambda i, c: (0, 0, 0, 0)),
+            ),
+            scratch_shapes=[pltpu.VMEM((896, 1024), BF16)],
+        ),
         out_shape=(
             jax.ShapeDtypeStruct((640, LON), F32),
             jax.ShapeDtypeStruct((2, 24, 8, 768), F32),
         ),
-        in_specs=[
-            pl.BlockSpec((640, 2048), lambda i: (0, 0)),
-            pl.BlockSpec((896, 2048), lambda i: (i, 0)),
-            pl.BlockSpec((4, 6, 2, 8, 768), lambda i: (0, 0, 0, 0, 0)),
-        ],
-        out_specs=(
-            pl.BlockSpec((640, 896), lambda i: (0, i)),
-            pl.BlockSpec((2, 24, 8, 768), lambda i: (0, 0, 0, 0)),
-        ),
         compiler_params=pltpu.CompilerParams(vmem_limit_bytes=LIMIT),
-    )(spread, angles, spectra)
+    )(firsts, rest, angles, angles, angles, angles, partial, spectra)
 
     return (grid_out.reshape(8, 80, LON), spectra)
 

time: 98 us -> 103 us (1.051)
  the two profiles are of different devices: /device:TPU:1 before, /device:TPU:100 now
where the time goes in v8:
time: 103 us; the launch traced here: 102 us
  Pallas kernels  100 us (97%)
  other arithmetic  1.27 us (1%)
    pallas_call x1, Pallas kernels, body(): pl.pallas_call(exchange_kernel, name='exchange', out_shape=(jax.ShapeDtyp...  87.9 us
    pallas_call x1, Pallas kernels, body(): pl.pallas_call(backward_kernel, name='backward', grid_spec=pltpu.Prefetch...  12.6 us

profile of v8, /device:TPU:100, one launch (start us, length us, event | category | flops | bytes accessed | tf_op | source)
XLA Modules:
  0.0 102.4 jit_solution(18201546669794283206)
XLA Ops:
  0.7 1.3 %fusion.firsts_ref = s32[2]{0:T(128)} fusion(s32[2]{0:T(128)} %constant.67.clone, s32[]{:T(128)S(6)} %select_n.28), kind=kLoop, calls=%fused_computation.8 | loop fusion | flops 66 | bytes 20 | tf_op jit(solution)/shard_map/add | solution.py:589
  1.9 87.9 %exchange.1 = (bf16[2688,2048]{1,0:T(8,128)(2,1)}, f32[640,2688]{1,0:T(8,128)}, bf16[640,1024]{1,0:T(8,128)(2,1)}, bf16[4,6,2,8,768]{4,3,2,1,0:T(8,128)(2,1)}) custom-call(s32[768]{0:T(1024)} %wave_ref.1, bf16[640,2688]{1,0:T(8,128)(2,1)} %bitcast.6, bf16[6,1280,768]{2,1,0:T(8,128)(2,1)} %tables_ref.1, f32[10,128]{1,0:T(8,128)} %bitcast.8, f32[1,32]{1,0:T(1,128)} %bitcast.9, ...), custom_call_target="tpu_custom_call" | custom-call | tf_op jit(solution)/shard_map/exchange/pallas_call | solution.py:536
  89.8 12.6 %backward.1 = (f32[640,2688]{1,0:T(8,128)}, f32[2,24,8,768]{3,2,1,0:T(8,128)}) custom-call(s32[2]{0:T(128)} %fusion.firsts_ref, bf16[640,1024]{1,0:T(8,128)(2,1)} %get-tuple-element.8.rest_ref, bf16[2688,2048]{1,0:T(8,128)(2,1)} %get-tuple-element.9.a_ref.b_ref.c_ref.d_ref, bf16[2688,2048]{1,0:T(8,128)(2,1)} %get-tuple-element.9.a_ref.b_ref.c_ref.d_ref, ...), custom_call_target="tpu_custom_call" | custom-call | tf_op jit(solution)/shard_map/backward/pallas_call | solution.py:594

commit v9 on v7

--- a/solution.py
+++ b/solution.py
@@ -124,7 +124,7 @@
     modes[...] = as_column(line[0:1])[0:80].astype(jnp.int32)
 
 
-def fill_trig(waves, trig):
+def fill_trig(waves, trig, groups):
     column = lax.rem(lanes(TRIG_ROWS), 16)
     row = lax.broadcasted_iota(jnp.int32, (TRIG_ROWS, 128), 0)
     first = row < ROW_A
@@ -134,14 +134,11 @@
     turn = jnp.where(first & (lax.rem(column, 2) == 1), LON // 4, 0)
     scale = jnp.where(first, jnp.where(column < 12, 1.0 / math.sqrt(LON), 0.0), 1.0)
 
-    def one(group, carry):
+    for group in groups:
         index = lax.rem(factor * waves[pl.ds(group, 1)] + turn, LON)
         radians = index.astype(F32) * (2.0 * math.pi / LON)
         trig[0, group] = jnp.cos(radians) * scale
         trig[1, group] = jnp.sin(radians) * scale
-        return carry
-
-    lax.fori_loop(0, GROUPS, one, 0)
 
 
 def make_table(trig, group, half, uv, table):
@@ -172,10 +169,10 @@
     lane16 = lax.rem(lanes(), 16)
     spread_waves(slots_ref, waves)
     spread_modes(modes_ref, line, modes)
-    fill_trig(waves, trig)
 
     def step_body(step, carry):
         groups = (group_at(2 * step), group_at(2 * step + 1))
+        fill_trig(waves, trig, groups)
         for half in range(2):
             make_table(trig, groups[half], half, uv, table)
         copies = [
@@ -362,7 +359,7 @@
             else:
                 pltpu.make_async_copy(source, target, spec_own).start()
 
-    mine = 2 * lax.rem(z, 2) + x // 2
+    mine, column = 2 * lax.rem(z, 2) + x // 2, z * 4 + x
     turn = flip_matrix(320)
     lane16 = lax.rem(lanes(), 16)
 
@@ -412,7 +409,7 @@
                 for k in range(4):
                     send_one(
                         i * 4 + k, wide.at[aligned(80 * i, 64), 128 * k : 128 * k + 128],
-                        inbox.at[me], send_sem, recv_sem.at[mine], own_sem,
+                        inbox.at[me], send_sem, recv_sem.at[column], own_sem,
                     )
             return carry
 
@@ -432,19 +429,20 @@
     for stage in range(4):
         kind = lax.rem(here + 4 - stage, 4)
 
-        @pl.when(kind == mine)
-        def _():
-            pltpu.make_async_copy(inbox.at[0], inbox.at[0], own_sem).wait()
-            arrived(31, kind)
-
-        @pl.when(kind != mine)
-        def _():
-            arrived(32, kind)
-
         first = (kind // 2) * 4 + 2 * lax.rem(kind, 2)
 
         def gather(n, carry):
             group = first + 8 * (n // 2) + lax.rem(n, 2)
+
+            @pl.when(group == column)
+            def _():
+                pltpu.make_async_copy(inbox.at[0], inbox.at[0], own_sem).wait()
+                arrived(7, group)
+
+            @pl.when(group != column)
+            def _():
+                arrived(8, group)
+
             wave = waves[pl.ds(group, 1)]
             cols = aligned(128 * group, 128, 128)
             for q in range(5):
@@ -460,12 +458,10 @@
                     spread[80 * f + 16 * q : 80 * f + 16 * q + 16, cols] = jnp.where(
                         keep, 2.0 * part, 0.0
                     ).astype(BF16)
+            pltpu.make_async_copy(spread.at[:, cols], spread_ref.at[:, cols], out_sem).start()
             return carry
 
         lax.fori_loop(0, 4, gather, 0)
-        for half in range(2):
-            cols = aligned(128 * first + 1024 * half, 256, 256)
-            pltpu.make_async_copy(spread.at[:, cols], spread_ref.at[:, cols], out_sem).start()
 
     pltpu.make_async_copy(spread, spread_ref, out_sem).wait()
     pltpu.make_async_copy(spec_ref.at[0], spec_ref.at[0], spec_own).wait()
@@ -538,7 +534,7 @@
         + [pltpu.SemaphoreType.DMA] * 9
         + [
             pltpu.SemaphoreType.DMA((2,)),
-            pltpu.SemaphoreType.DMA((4,)),
+            pltpu.SemaphoreType.DMA((GROUPS,)),
             pltpu.SemaphoreType.DMA((6,)),
         ],
         compiler_params=pltpu.CompilerParams(

time: 98 us -> 97.8 us (level)
  no operation moved by 1% of the time
where the time goes in v9:
time: 97.8 us; the launch traced here: 96.7 us
  Pallas kernels  96 us (98%)
    pallas_call x1, Pallas kernels, body(): pl.pallas_call(exchange_kernel, name='exchange', out_shape=(jax.ShapeDtyp...  82.5 us
    pallas_call x1, Pallas kernels, body(): pl.pallas_call(backward_kernel, name='backward', grid=(3,), out_shape=(ja...  13.5 us

profile of v9, /device:TPU:1, one launch (start us, length us, event | category | flops | bytes accessed | tf_op | source)
XLA Modules:
  0.0 96.7 jit_solution(2074119925812534117)
XLA Ops:
  0.6 82.5 %exchange.1 = (bf16[2688,2048]{1,0:T(8,128)(2,1)}, bf16[640,2048]{1,0:T(8,128)(2,1)}, bf16[4,6,2,8,768]{4,3,2,1,0:T(8,128)(2,1)}) custom-call(s32[768]{0:T(1024)} %wave_ref.1, bf16[640,2688]{1,0:T(8,128)(2,1)} %bitcast.6, bf16[6,1280,768]{2,1,0:T(8,128)(2,1)} %tables_ref.1, f32[10,128]{1,0:T(8,128)} %bitcast.8, f32[1,32]{1,0:T(1,128)} %bitcast.9, ...), custom_call_target="tpu_custom_call" | custom-call | tf_op jit(solution)/shard_map/exchange/pallas_call | solution.py:501
  83.2 13.5 %backward.1 = (f32[640,2688]{1,0:T(8,128)}, f32[2,24,8,768]{3,2,1,0:T(8,128)}) custom-call(bf16[640,2048]{1,0:T(8,128)(2,1)} %get-tuple-element.7.spread_ref, bf16[2688,2048]{1,0:T(8,128)(2,1)} %get-tuple-element.8.angles_ref, bf16[4,6,2,8,768]{4,3,2,1,0:T(8,128)(2,1)} %get-tuple-element.9.spec_ref), custom_call_target="tpu_custom_call" | custom-call | tf_op jit(solution)/shard_map/backward/pallas_call | solution.py:548
